TPU v7x, 128 devices: a whole 4x4x4 slice. The times are simulated.
128 devices in a mesh: leaf: 128 (over z, x, y, core).
Axes of the slice: x: 4, y: 4, z: 4, core: 2. Of those that a mesh axis runs over, the one named last changes fastest.
Arguments:
- coords: float32 [3, 1048576], P(None, 'leaf'), may hold values from 0 to 1
- charges: bfloat16 [1048576, 128], P('leaf'), may hold values from -6 to 6
- near_leaves: int32 [8192, 27], P('leaf'), may hold values from 0 to 191
- leaf_basis: bfloat16 [8192, 4096], P('leaf'), may hold values from -1 to 1
- leaf_transfer: bfloat16 [8192, 1024], P('leaf'), may hold values from -0.75 to 0.75
- mid_transfer: bfloat16 [1024, 1024], P('leaf'), may hold values from -0.75 to 0.75
- base_transfer: bfloat16 [128, 1024], P('leaf'), may hold values from -0.75 to 0.75
- base_coupling: bfloat16 [24192, 1024], P('leaf'), may hold values from -0.01953125 to 0.01953125
- base_target: int32 [24192, 1], P('leaf'), may hold values from 0 to 127; in each aligned block of 189 rows (0 to 188, 189 to 377, ...) at most 2 rows name the same one
- base_source: int32 [24192], P('leaf'), may hold values from 0 to 127
- top_coupling: bfloat16 [1024, 1024], P('leaf'), may hold values from -0.015625 to 0.015625
- top_target: int32 [1024], P('leaf'), may hold values from 0 to 15
- top_source: int32 [1024], P('leaf'), may hold values from 0 to 15
Outputs:
- potential: bfloat16 [1048576, 128], P('leaf')
Inputs may be any that keep to these rules, and one draw needn't show every extreme that they name: `near_leaves`: entry j of leaf l names leaf 64 * (l // 64 - 1) + j: a leaf of the device before in Morton order, of the row's own device, or of the device after; repeats may occur. `base_target`: among the 189 blocks of one device no base cluster is the target more than 2 times; that count is reached.
All inputs are finite; a program needn't handle non-finite values.
Results may differ from a plain program's by a relative error of at most 0.01.
Values may be sent and summed in bfloat16 or wider, within the bound.
No kernel may reach another device: no remote copies, remote signals or barrier semaphores. Data moves between devices by JAX's collectives and lax.ppermute only.
A program may use at most 128 MiB of HBM per device.

v0:
```python
import math

import jax
import jax.numpy as jnp
from jax import lax
from jax.experimental import pallas as pl
from jax.experimental.pallas import tpu as pltpu
from jax.sharding import Mesh
from jax.sharding import PartitionSpec as P

K = 32
RHS = 128
M = 128
NNEAR = 27
LEAVES_DEV = 64
MIDS_DEV = 8
NBASE = 128
CHIPS = 64
NTOP = 16
BLK_DEV = 189
BLK_PAD = 192
TOPB_DEV = 8
FEAT = 48
POINTS = 8192
TAIL = 576
MSG = 48
LEAF = ("leaf_0", "leaf_1", "leaf_2", "leaf_3")
delta_sq = 0.0025
near_scale_sq = float(NNEAR * M)

f32 = jnp.float32
bf16 = jnp.bfloat16


def in_vmem():
    return pl.BlockSpec(memory_space=pltpu.VMEM)


def in_smem():
    return pl.BlockSpec(memory_space=pltpu.SMEM)


def in_place():
    return pl.BlockSpec(memory_space=pl.ANY)


def stacked_groups(tile):
    tile = tile.astype(f32)
    group = lax.broadcasted_iota(jnp.int32, tile.shape, 1) // K
    return jnp.concatenate([jnp.where(group == g, tile, 0.0) for g in range(4)], axis=0)


def rolled_groups(tile):
    tile = tile.astype(f32)
    lane = lax.broadcasted_iota(jnp.int32, tile.shape, 1)
    parts = [tile] + [pltpu.roll(tile, 128 - K * g, 1) for g in range(1, 4)]
    return jnp.concatenate([jnp.where(lane < K, part, 0.0) for part in parts], axis=0)


def unpermute(rows):
    to = lax.broadcasted_iota(jnp.int32, (K, K), 0)
    at = lax.broadcasted_iota(jnp.int32, (K, K), 1)
    order = jnp.where(to == 4 * (at % 8) + at // 8, 1.0, 0.0).astype(bf16)
    return jnp.dot(order, rows.astype(bf16), preferred_element_type=f32).astype(bf16)


def four_times(rows):
    return jnp.concatenate([rows] * 4, axis=0)


def up_kernel(
    q, coords, basis, leaf_rows, mid_rows, lift_rows, message, v_rows, halo,
    basis_s, leaf_s, mid_s, lift_s, points_s, tail_s, sems,
):
    bulk = pltpu.make_async_copy(q, halo.at[pl.ds(0, POINTS)], sems.at[0])
    bulk.start()

    def spread(g, carry):
        row = coords[:, pl.ds(pl.multiple_of(g * M, M), M)]
        points_s[pl.ds(g, 3, stride=LEAVES_DEV), :] = row
        return carry

    lax.fori_loop(0, LEAVES_DEV, spread, 0, unroll=8)
    for i, piece in enumerate(pieces(points_s[...])):
        tail_s[pl.ds(i * 3 * LEAVES_DEV, 3 * LEAVES_DEV), :] = piece.astype(bf16)
    tail = pltpu.make_async_copy(tail_s, halo.at[pl.ds(POINTS, TAIL)], sems.at[1])
    tail.start()

    for i in range(8):
        piece = pl.ds(i * 128, 128)
        mid_s[pl.ds(i, MIDS_DEV, stride=8), :] = mid_rows[:, piece].astype(f32)
        lift_s[pl.ds(i, 1), :] = lift_rows[:, piece].astype(f32)
    lift = lift_s[pl.ds(0, 8), :]
    straight = unpermute(rolled_groups(lift)).astype(f32)
    turned = jnp.concatenate([straight, jnp.zeros((96, 128), f32)], axis=0).T
    lift_t = turned[:8]
    for g in range(1, 4):
        lift_t = lift_t + pltpu.roll(turned[8 * g : 8 * g + 8], K * g, 1)

    coeffs = jnp.zeros((K, RHS), f32)
    for m in range(MIDS_DEV):
        own = pl.ds(8 * m, 8)
        for i in range(8):
            leaf_s[pl.ds(64 * m + i, 8, stride=8), :] = leaf_rows[own, pl.ds(i * 128, 128)].astype(f32)
        for k in range(K):
            at = 256 * m + 8 * (k % 4) + k // 4
            basis_s[pl.ds(at, 8, stride=K), :] = basis[own, pl.ds(k * M, M)].astype(f32)
        mid = four_times(unpermute(rolled_groups(mid_s[pl.ds(8 * m, 8), :])))
        lhs = [stacked_groups(leaf_s[pl.ds(64 * m + 8 * c, 8), :]) for c in range(8)]
        lhs = jnp.concatenate(lhs, axis=0).astype(bf16)
        through = jnp.dot(lhs, mid, preferred_element_type=f32)
        rows = []
        for c in range(8):
            back = through[K * c : K * (c + 1)].T[:K].astype(bf16)
            own_basis = basis_s[pl.ds(256 * m + K * c, K), :].astype(bf16)
            rows.append(jnp.dot(back, own_basis, preferred_element_type=f32))
        for h in range(2):
            four = jnp.concatenate(rows[4 * h : 4 * h + 4], axis=0)
            v_rows[2 * m + h] = four.T.astype(bf16)
        across = jnp.concatenate([row.astype(bf16) for row in rows], axis=1)
        coeffs = coeffs + jnp.dot(
            across, q[pl.ds(8 * m * M, 8 * M)], preferred_element_type=f32
        )
    whole = jnp.concatenate([coeffs, lift, lift_t], axis=0).astype(bf16)

    def put(d, carry):
        message[d] = whole
        return carry

    lax.fori_loop(0, CHIPS, put, 0, unroll=8)
    bulk.wait()
    tail.wait()


def couple_kernel(
    core, table, sources, top_target, top_source, mine, other, tiles, top_tiles, out,
    gathered, top_sum, top_rows, sems,
):
    me = core[0]
    copies = [
        pltpu.make_async_copy(mine, gathered.at[pl.ds(me * CHIPS, CHIPS)], sems.at[0]),
        pltpu.make_async_copy(other, gathered.at[pl.ds((1 - me) * CHIPS, CHIPS)], sems.at[1]),
    ]
    for copy in copies:
        copy.start()
    for copy in copies:
        copy.wait()
    top_sum[...] = jnp.zeros((NTOP, K, RHS), f32)
    lifted = []
    for b in range(TOPB_DEV):
        source = top_source[b]
        lhs, rhs = [], []
        for c in range(8):
            child = gathered[(c % 2) * CHIPS + source * 4 + c // 2]
            lhs.append(stacked_groups(child[40:48]))
            rhs.append(four_times(child[:K]))
        lifted.append(
            jnp.dot(
                jnp.concatenate(lhs, axis=1).astype(bf16),
                jnp.concatenate(rhs, axis=0),
                preferred_element_type=f32,
            ).astype(bf16)
        )
    products = [
        jnp.dot(
            stacked_groups(top_tiles[b]).astype(bf16),
            four_times(lifted[b]),
            preferred_element_type=f32,
        )
        for b in range(TOPB_DEV)
    ]
    for b in range(TOPB_DEV):
        target = top_target[b]
        top_sum[target] = top_sum[target] + products[b]
    every = jnp.concatenate([top_sum[t] for t in range(NTOP)], axis=1)
    every = unpermute(every)
    for t in range(NTOP):
        top_rows[t] = every[:, t * RHS : (t + 1) * RHS]

    def one(d, carry):
        lhs, rhs = [], []
        for row in (0, 1):
            b = table[row, d]
            s = sources[b]
            lhs.append(stacked_groups(tiles[b]))
            rhs.append(four_times(gathered[(s % 2) * CHIPS + s // 2, :K]))
        lhs.append(stacked_groups(gathered[(d % 2) * CHIPS + d // 2, 32:40]))
        rhs.append(four_times(top_rows[d // 8]))
        out[d] = jnp.dot(
            jnp.concatenate(lhs, axis=1).astype(bf16),
            jnp.concatenate(rhs, axis=0),
            preferred_element_type=f32,
        ).astype(bf16)
        return carry

    lax.fori_loop(0, NBASE, one, 0, unroll=16)


def pieces(values):
    high = values.astype(bf16).astype(f32)
    rest = values - high
    middle = rest.astype(bf16).astype(f32)
    low = (rest - middle).astype(bf16).astype(f32)
    return high, middle, low


def features(points, source):
    row = lax.broadcasted_iota(jnp.int32, (8, M), 0)
    padded = jnp.concatenate([points, jnp.zeros((5, M), f32)], axis=0)
    centred = jnp.where(row < 3, (padded - 0.5) * math.sqrt(near_scale_sq), 0.0)
    norm = jnp.sum(centred * centred, axis=0, keepdims=True)
    if source:
        norm = norm + delta_sq * near_scale_sq
    norm = jnp.broadcast_to(norm, (8, M))
    high, middle, low = pieces(centred)
    norms = pieces(norm)
    one = jnp.ones((8, M), f32)
    if source:
        groups = [high, middle, high, low, high, middle]
    else:
        groups = [-2 * high, -2 * high, -2 * middle, -2 * high, -2 * low, -2 * middle]
    done = []
    for i, part in enumerate(groups):
        if i < 3:
            third, fourth = (one, norms[i]) if source else (norms[i], one)
            part = jnp.where(row == 3, third, jnp.where(row == 4, fourth, part))
        done.append(part)
    return jnp.concatenate(done, axis=0)


def early_kernel(base_target, coords, table, feats, aims):
    targets = base_target[...]
    block = lax.broadcasted_iota(jnp.int32, (BLK_DEV, NBASE), 0)
    here = targets == lax.broadcasted_iota(jnp.int32, (BLK_DEV, NBASE), 1)
    first = jnp.min(jnp.where(here, block, BLK_DEV), axis=0, keepdims=True)
    last = jnp.max(jnp.where(here, block, -1), axis=0, keepdims=True)
    table[...] = jnp.zeros((8, NBASE), jnp.int32)
    table[0:1] = first
    table[1:2] = jnp.where(last > first, last, BLK_DEV)

    def prepare(g, carry):
        points = coords[:, pl.ds(pl.multiple_of(g * M, M), M)]
        feats[g] = features(points, True).astype(bf16)
        aims[g] = features(points, False).T.astype(bf16)
        return carry

    lax.fori_loop(0, LEAVES_DEV, prepare, 0, unroll=8)


def near_kernel(
    columns, own_feats, own_aims, before, own, after, out,
    pool, feats, aims, tails, points_s, kernel_a, kernel_b, sems,
):
    L = LEAVES_DEV
    tail_copies = [
        pltpu.make_async_copy(part.at[pl.ds(POINTS, TAIL)], tails.at[i], sems.at[i])
        for i, part in enumerate((before, after))
    ]
    copies = [
        pltpu.make_async_copy(own_aims, aims, sems.at[2]),
        pltpu.make_async_copy(own_feats, feats.at[pl.ds(L, L)], sems.at[3]),
    ]
    copies += [
        pltpu.make_async_copy(
            part.at[pl.ds(0, POINTS)], pool.at[pl.ds(i * POINTS, POINTS)], sems.at[4 + i]
        )
        for i, part in enumerate((before, own, after))
    ]
    for copy in tail_copies + copies:
        copy.start()
    for i in range(2):
        tail_copies[i].wait()
        part = [tails[i, pl.ds(p * 3 * L, 3 * L)].astype(f32) for p in range(3)]
        points_s[i] = part[0] + part[1] + part[2]

        def prepare(g, carry, i=i):
            points = points_s[i, pl.ds(g, 3, stride=L), :]
            feats[2 * i * L + g] = features(points, True).astype(bf16)
            return carry

        lax.fori_loop(0, L, prepare, 0, unroll=8)
    for copy in copies:
        copy.wait()

    def weigh(l, store):
        mine = aims[l]
        for j in range(0, NNEAR, 2):
            named = [columns[l * NNEAR + k] for k in range(j, min(j + 2, NNEAR))]
            theirs = jnp.concatenate([feats[g] for g in named], axis=1)
            squares = jnp.dot(mine, theirs, preferred_element_type=f32)
            store[:, pl.ds(j * M, len(named) * M)] = lax.rsqrt(squares).astype(bf16)

    def apply(l, store):
        starts = [pl.multiple_of(columns[l * NNEAR + j] * M, M) for j in range(NNEAR)]
        named = jnp.concatenate([pool[pl.ds(start, M)] for start in starts], axis=0)
        out[l] = jnp.dot(store[...], named, preferred_element_type=f32)

    weigh(0, kernel_a)

    def two(i, carry):
        weigh(2 * i + 1, kernel_b)
        apply(2 * i, kernel_a)
        weigh(jnp.minimum(2 * i + 2, L - 1), kernel_a)
        apply(2 * i + 1, kernel_b)
        return carry

    lax.fori_loop(0, L // 2, two, 0)


def down_kernel(parts, v_rows, near, out, parts_s, v_s, near_s, out_s, sems):
    steps = LEAVES_DEV // 8
    chunks = [pl.ds(8 * i, 8) for i in range(steps)]
    first = [
        pltpu.make_async_copy(parts, parts_s, sems.at[0]),
        pltpu.make_async_copy(v_rows, v_s, sems.at[1]),
    ]
    loads = [
        pltpu.make_async_copy(near.at[c], near_s.at[c], sems.at[2 + i])
        for i, c in enumerate(chunks)
    ]
    for copy in first + loads:
        copy.start()
    to = lax.broadcasted_iota(jnp.int32, (K, NBASE * K), 0)
    at = lax.broadcasted_iota(jnp.int32, (K, NBASE * K), 1) % K
    order = jnp.where(to == 4 * (at % 8) + at // 8, 1.0, 0.0).astype(bf16)
    first[0].wait()
    field = jnp.dot(order, parts_s[...].reshape(NBASE * K, RHS), preferred_element_type=f32)
    zero = jnp.zeros((K, RHS), f32)
    spread = [
        jnp.concatenate([field if g == h else zero for h in range(4)], axis=0) for g in range(4)
    ]
    spread = jnp.concatenate(spread, axis=1).astype(bf16)
    first[1].wait()
    stores = []
    for i, chunk in enumerate(chunks):
        rows = v_s[pl.ds(2 * i, 2)].reshape(2 * M, 4 * K)
        far = jnp.dot(rows, spread, preferred_element_type=f32)
        loads[i].wait()
        for c in range(8):
            h, g = c // 4, c % 4
            part = far[h * M : (h + 1) * M, g * RHS : (g + 1) * RHS]
            out_s[8 * i + c] = (near_s[8 * i + c] + part).astype(bf16)
        stores.append(pltpu.make_async_copy(out_s.at[chunk], out.at[chunk], sems.at[10 + i]))
        stores[-1].start()
    for copy in stores:
        copy.wait()


def all_steps(
    coords, charges, near_leaves, leaf_basis, leaf_transfer, mid_transfer, base_transfer,
    base_coupling, base_target, base_source, top_coupling, top_target, top_source,
):
    L = LEAVES_DEV
    size = lax.axis_size(LEAF)
    up = [(i, i + 1) for i in range(size - 1)]
    down = [(j, i) for i, j in up]
    message, v_rows, halo = pl.pallas_call(
        up_kernel,
        out_shape=(
            jax.ShapeDtypeStruct((CHIPS, MSG, RHS), bf16),
            jax.ShapeDtypeStruct((L // 4, M, 4 * K), bf16),
            jax.ShapeDtypeStruct((POINTS + TAIL, RHS), bf16),
        ),
        in_specs=[in_vmem()] * 6,
        out_specs=(in_vmem(), in_vmem(), in_place()),
        scratch_shapes=[
            pltpu.VMEM((L * K, M), f32),
            pltpu.VMEM((L * 8, 128), f32),
            pltpu.VMEM((MIDS_DEV * 8, 128), f32),
            pltpu.VMEM((8, 128), f32),
            pltpu.VMEM((3 * L, M), f32),
            pltpu.VMEM((TAIL, M), bf16),
            pltpu.SemaphoreType.DMA((2,)),
        ],
        name="up",
        cost_estimate=pl.CostEstimate(flops=2 * 10**9, bytes_accessed=5 * 10**6, transcendentals=0),
    )(charges, coords, leaf_basis, leaf_transfer, mid_transfer, base_transfer)
    mine = lax.all_to_all(message, LEAF[:3], 0, 0, tiled=True)
    other = lax.ppermute(mine, LEAF[3], [(0, 1), (1, 0)])
    before = lax.ppermute(halo, LEAF, up)
    after = lax.ppermute(halo, LEAF, down)

    table, own_feats, own_aims = pl.pallas_call(
        early_kernel,
        out_shape=(
            jax.ShapeDtypeStruct((8, NBASE), jnp.int32),
            jax.ShapeDtypeStruct((L, FEAT, M), bf16),
            jax.ShapeDtypeStruct((L, M, FEAT), bf16),
        ),
        in_specs=[in_vmem()] * 2,
        out_specs=(in_vmem(),) * 3,
        name="early",
        cost_estimate=pl.CostEstimate(flops=10**9, bytes_accessed=10**6, transcendentals=0),
    )(base_target, coords)

    spare = BLK_PAD - BLK_DEV
    tiles = jnp.pad(base_coupling, ((0, spare), (0, 0))).reshape(BLK_PAD, 8, 128)
    sources = jnp.pad(base_source, (0, spare))
    partial = pl.pallas_call(
        couple_kernel,
        out_shape=jax.ShapeDtypeStruct((NBASE, K, RHS), bf16),
        in_specs=[in_smem()] * 5 + [in_place()] * 2 + [in_vmem()] * 2,
        out_specs=in_vmem(),
        scratch_shapes=[
            pltpu.VMEM((NBASE, MSG, RHS), bf16),
            pltpu.VMEM((NTOP, K, RHS), f32),
            pltpu.VMEM((NTOP, K, RHS), bf16),
            pltpu.SemaphoreType.DMA((2,)),
        ],
        name="couple",
        cost_estimate=pl.CostEstimate(flops=2 * 10**9, bytes_accessed=5 * 10**6, transcendentals=0),
    )(
        lax.axis_index(LEAF[3]).reshape(1).astype(jnp.int32),
        table,
        sources,
        top_target,
        top_source,
        mine,
        other,
        tiles,
        top_coupling.reshape(TOPB_DEV, 8, 128),
    )
    parts = lax.all_to_all(partial, LEAF, 0, 0, tiled=True)

    near = pl.pallas_call(
        near_kernel,
        out_shape=jax.ShapeDtypeStruct((L, M, RHS), f32),
        in_specs=[in_smem()] + [in_place()] * 5,
        out_specs=in_vmem(),
        scratch_shapes=[
            pltpu.VMEM((3 * POINTS, RHS), bf16),
            pltpu.VMEM((3 * L, FEAT, M), bf16),
            pltpu.VMEM((L, M, FEAT), bf16),
            pltpu.VMEM((2, TAIL, M), bf16),
            pltpu.VMEM((2, 3 * L, M), f32),
            pltpu.VMEM((M, NNEAR * M), bf16),
            pltpu.VMEM((M, NNEAR * M), bf16),
            pltpu.SemaphoreType.DMA((7,)),
        ],
        name="near",
        cost_estimate=pl.CostEstimate(
            flops=4 * 10**10, bytes_accessed=10**7, transcendentals=3 * 10**7
        ),
    )(near_leaves.reshape(-1), own_feats, own_aims, before, charges, after)

    potential = pl.pallas_call(
        down_kernel,
        out_shape=jax.ShapeDtypeStruct((L, M, RHS), bf16),
        in_specs=[in_place()] * 3,
        out_specs=in_place(),
        scratch_shapes=[
            pltpu.VMEM((NBASE, K, RHS), bf16),
            pltpu.VMEM((L // 4, M, 4 * K), bf16),
            pltpu.VMEM((L, M, RHS), f32),
            pltpu.VMEM((L, M, RHS), bf16),
            pltpu.SemaphoreType.DMA((18,)),
        ],
        name="down",
        cost_estimate=pl.CostEstimate(flops=10**9, bytes_accessed=10**7, transcendentals=0),
    )(parts, v_rows, near)
    return potential.reshape(L * M, RHS)


def solution(mesh):
    split = Mesh(mesh.devices.reshape(4, 4, 4, 2), LEAF)
    by_leaf = P(LEAF, None)
    in_specs = (P(None, LEAF),) + (by_leaf,) * 8 + (P(LEAF), by_leaf, P(LEAF), P(LEAF))
    return jax.shard_map(
        all_steps, mesh=split, in_specs=in_specs, out_specs=by_leaf, check_vma=False
    )
```

profile of v0, /device:TPU:0, one launch (start us, length us, event | category | flops | bytes accessed | tf_op | source)
XLA Modules:
  0.0 128.5 jit_solution(3593171923114730346)
XLA Ops:
  0.0 0.0 copy-start.5
  0.0 0.0 copy-start.3
  0.0 0.0 copy-start.2
  0.0 7.7 %up.1 = (bf16[64,48,128]{2,1,0:T(8,128)(2,1)}, bf16[16,128,128]{2,1,0:T(8,128)(2,1)}, bf16[8768,128]{1,0:T(8,128)(2,1)}) custom-call(bf16[8192,128]{1,0:T(8,128)(2,1)} %own.1, f32[3,8192]{1,0:T(4,128)} %coords.3, bf16[64,4096]{1,0:T(8,128)(2,1)} %basis.1, bf16[64,1024]{1,0:T(8,128)(2,1)} %leaf_rows.1, bf16[8,1024]{1,0:T(8,128)(2,1)} %mid_rows.1, ...), custom_call_target="tpu_custom_call" | custom-call | flops 2000000000 | bytes 5000000 | tf_op jit(solution)/shard_map/up/pallas_call | solution.py:357
  7.7 0.0 copy-start.4
  7.7 0.0 copy-start.6
  7.7 1.4 %collective-permute-start.1 = (bf16[8768,128]{1,0:T(8,128)(2,1)}, bf16[8768,128]{1,0:T(8,128)(2,1)S(1)}, u32[]{:S(2)}, u32[]{:S(2)}) collective-permute-start(bf16[8768,128]{1,0:T(8,128)(2,1)} %get-tuple-element.16), channel_id=1, source_target_pairs={{0,1},{1,2},{2,3},{3,4},{4,5},{5,6},{6,7},{7,8},{8,9},{9,10},{10,1... | collective-permute-start | bytes 6733832 | tf_op jit(solution)/shard_map/ppermute | solution.py:380
  9.1 1.3 %collective-permute-start.2 = (bf16[8768,128]{1,0:T(8,128)(2,1)}, bf16[8768,128]{1,0:T(8,128)(2,1)}, u32[]{:S(2)}, u32[]{:S(2)}) collective-permute-start(bf16[8768,128]{1,0:T(8,128)(2,1)} %get-tuple-element.16), channel_id=1, source_target_pairs={{1,0},{2,1},{3,2},{4,3},{5,4},{6,5},{7,6},{8,7},{9,8},{10,9},{11,1... | collective-permute-start | bytes 6733832 | tf_op jit(solution)/shard_map/ppermute | solution.py:381
  10.4 45.3 %all_to_all.10.mine = bf16[64,48,128]{2,1,0:T(8,128)(2,1)S(1)} all-to-all(bf16[64,48,128]{2,1,0:T(8,128)(2,1)} %get-tuple-element.12), channel_id=1, replica_groups=mesh['leaf_0'=4,'leaf_1'=4,'leaf_2'=4,'leaf_3'=2] {'leaf_0','leaf_1','le..., dimensions={0} | all-to-all | bytes 1572864 | tf_op jit(solution)/shard_map/all_to_all | solution.py:378
  55.8 0.0 copy-start.1
  55.8 0.0 collective-permute-start
  55.8 0.0 copy-done.5
  55.8 0.9 copy.15.base_target
  56.7 0.0 copy-done.3
  56.7 0.1 copy.16
  56.8 0.7 reshape.18.columns
  57.5 0.0 copy-done.2
  57.5 0.8 copy.17
  58.4 0.0 copy-done.4
  58.4 0.6 copy.20
  59.0 0.0 copy-done.6
  59.0 0.6 pad.8.sources
  59.5 3.8 %early.1 = (s32[8,128]{1,0:T(8,128)}, bf16[64,48,128]{2,1,0:T(8,128)(2,1)}, bf16[64,128,48]{2,1,0:T(8,128)(2,1)}) custom-call(s32[189,1]{1,0:T(8,128)} %copy.15.base_target, f32[3,8192]{1,0:T(4,128)} %coords.3), custom_call_target="tpu_custom_call" | custom-call | flops 1000000000 | bytes 1000000 | tf_op jit(solution)/shard_map/early/pallas_call | solution.py:383
  63.4 0.0 copy-done.1
  63.4 0.0 collective-permute-done.other
  63.4 8.4 %couple.1 = bf16[128,32,128]{2,1,0:T(8,128)(2,1)} custom-call(s32[1]{0:T(128)} %bitcast.core, s32[8,128]{1,0:T(8,128)} %get-tuple-element.11.table, s32[192]{0:T(256)} %pad.8.sources, s32[8]{0:T(128)} %top_target.1, s32[8]{0:T(128)} %top_source.1, bf16[64,48,128]{2,1,0:T(8,128)(2,1)} %copy-done.1, bf16[64,48,128]{2,1,0:T(8,128)(2,1)} %collective-permute-done.other, ...), custom_call_target="tpu_custom_call" | custom-call | flops 2000000000 | bytes 5000000 | tf_op jit(solution)/shard_map/couple/pallas_call | solution.py:399
  71.8 9.2 %all-to-all-start.1 = ((bf16[128,32,128]{2,1,0:T(8,128)(2,1)}), bf16[128,32,128]{2,1,0:T(8,128)(2,1)S(1)}, u32[]{:S(2)}, u32[]{:S(2)}) async-start(bf16[128,32,128]{2,1,0:T(8,128)(2,1)} %couple.1), calls=%async_computation.1 | async-start | bytes 2097152 | tf_op jit(solution)/shard_map/all_to_all | solution.py:423
  81.0 0.0 collective-permute-done.1.before
  81.0 0.0 copy-start.7
  81.0 0.0 collective-permute-done.2.after
  81.0 1.4 %copy-done.7 = bf16[8768,128]{1,0:T(8,128)(2,1)} copy-done((bf16[8768,128]{1,0:T(8,128)(2,1)}, bf16[8768,128]{1,0:T(8,128)(2,1)S(1)}, u32[]{:S(2)}) %copy-start.7) | copy-done | bytes 2244632
  82.5 41.0 %near.1 = f32[64,128,128]{2,1,0:T(8,128)} custom-call(s32[1728]{0:T(1024)} %reshape.18.columns, bf16[64,48,128]{2,1,0:T(8,128)(2,1)} %get-tuple-element.14.own_feats, bf16[64,128,48]{2,1,0:T(8,128)(2,1)} %get-tuple-element.15.own_aims, bf16[8768,128]{1,0:T(8,128)(2,1)} %copy-done.7, bf16[8192,128]{1,0:T(8,128)(2,1)} %own.1, ...), custom_call_target="tpu_custom_call" | custom-call | flops 40000000000 | bytes 10000000 | tf_op jit(solution)/shard_map/near/pallas_call | solution.py:425
  123.4 0.0 all-to-all-done.1.parts
  123.4 0.0 copy-start
  123.4 1.0 copy-done
  124.4 4.1 %down.1 = bf16[64,128,128]{2,1,0:T(8,128)(2,1)} custom-call(bf16[128,32,128]{2,1,0:T(8,128)(2,1)} %copy-done, bf16[16,128,128]{2,1,0:T(8,128)(2,1)} %get-tuple-element.13.v_rows, f32[64,128,128]{2,1,0:T(8,128)} %near.1), custom_call_target="tpu_custom_call" | custom-call | flops 1000000000 | bytes 10000000 | tf_op jit(solution)/shard_map/down/pallas_call | solution.py:446
  (1 shorter events, 0.0 us)
Async XLA Ops:
  0.0 55.8 %copy-start.5 = (s32[189,1]{0,1:T(1,128)S(1)}, s32[189,1]{0,1:T(1,128)}, u32[]{:S(2)}) copy-start(s32[189,1]{0,1:T(1,128)} %param.21) | copy-start | bytes 2272
  0.0 56.7 %copy-start.3 = (s32[64,27]{0,1:T(8,128)S(1)}, s32[64,27]{0,1:T(8,128)}, u32[]{:S(2)}) copy-start(s32[64,27]{0,1:T(8,128)} %param.15) | copy-start | bytes 20740
  0.0 57.5 %copy-start.2 = (bf16[189,1024]{1,0:T(8,128)(2,1)S(1)}, bf16[189,1024]{1,0:T(8,128)(2,1)}, u32[]{:S(2)}) copy-start(bf16[189,1024]{1,0:T(8,128)(2,1)} %param.20) | copy-start | bytes 1161220
  7.7 50.7 %copy-start.4 = (bf16[8,1024]{1,0:T(8,128)(2,1)S(1)}, bf16[8,1024]{1,0:T(8,128)(2,1)}, u32[]{:S(2)}) copy-start(bf16[8,1024]{1,0:T(8,128)(2,1)} %param.23) | copy-start | bytes 49156
  7.7 51.3 %copy-start.6 = (s32[189]{0:T(256)S(1)}, s32[189]{0:T(256)}, u32[]{:S(2)}) copy-start(s32[189]{0:T(256)} %param.22) | copy-start | bytes 2272
  7.7 73.3 %collective-permute-start.1 = (bf16[8768,128]{1,0:T(8,128)(2,1)}, bf16[8768,128]{1,0:T(8,128)(2,1)S(1)}, u32[]{:S(2)}, u32[]{:S(2)}) collective-permute-start(bf16[8768,128]{1,0:T(8,128)(2,1)} %get-tuple-element.16), channel_id=1, source_target_pairs={{0,1},{1,2},{2,3},{3,4},{4,5},{5,6},{6,7},{7,8},{8,9},{9,10},{10,1... | collective-permute-start | bytes 6733832 | tf_op jit(solution)/shard_map/ppermute | solution.py:380
  9.1 71.9 %collective-permute-start.2 = (bf16[8768,128]{1,0:T(8,128)(2,1)}, bf16[8768,128]{1,0:T(8,128)(2,1)}, u32[]{:S(2)}, u32[]{:S(2)}) collective-permute-start(bf16[8768,128]{1,0:T(8,128)(2,1)} %get-tuple-element.16), channel_id=1, source_target_pairs={{1,0},{2,1},{3,2},{4,3},{5,4},{6,5},{7,6},{8,7},{9,8},{10,9},{11,1... | collective-permute-start | bytes 6733832 | tf_op jit(solution)/shard_map/ppermute | solution.py:381
  55.8 7.6 %copy-start.1 = (bf16[64,48,128]{2,1,0:T(8,128)(2,1)}, bf16[64,48,128]{2,1,0:T(8,128)(2,1)S(1)}, u32[]{:S(2)}) copy-start(bf16[64,48,128]{2,1,0:T(8,128)(2,1)S(1)} %all_to_all.10.mine) | copy-start | bytes 2359300
  55.8 7.6 %collective-permute-start = (bf16[64,48,128]{2,1,0:T(8,128)(2,1)S(1)}, bf16[64,48,128]{2,1,0:T(8,128)(2,1)}, u32[]{:S(2)}, u32[]{:S(2)}) collective-permute-start(bf16[64,48,128]{2,1,0:T(8,128)(2,1)S(1)} %all_to_all.10.mine), channel_id=1, source_target_pairs={{0,1},{1,0},{2,3},{3,2},{4,5},{5,4},{6,7},{7,6},{8,9},{9,8},{10,11... | collective-permute-start | bytes 2359304 | tf_op jit(solution)/shard_map/ppermute | solution.py:379
  71.8 51.7 %all-to-all-start.1 = ((bf16[128,32,128]{2,1,0:T(8,128)(2,1)}), bf16[128,32,128]{2,1,0:T(8,128)(2,1)S(1)}, u32[]{:S(2)}, u32[]{:S(2)}) async-start(bf16[128,32,128]{2,1,0:T(8,128)(2,1)} %couple.1), calls=%async_computation.1 | async-start | bytes 2097152 | tf_op jit(solution)/shard_map/all_to_all | solution.py:423
  81.0 1.4 %copy-start.7 = (bf16[8768,128]{1,0:T(8,128)(2,1)}, bf16[8768,128]{1,0:T(8,128)(2,1)S(1)}, u32[]{:S(2)}) copy-start(bf16[8768,128]{1,0:T(8,128)(2,1)S(1)} %collective-permute-done.1.before) | copy-start | bytes 6733828
  123.4 1.0 copy-start
where the time goes:
time: 129 us
  Pallas kernels  64.9 us (50%)
  blocking collectives  45.3 us (35%)
  starting transfers between devices  12 us (9%)
  local copies, waits for them, and re-layouts  6.14 us (5%)
    all_to_all x1, blocking collectives, all_steps(): mine = lax.all_to_all(message, LEAF[:3], 0, 0, tiled=True)  45.3 us
    pallas_call x1, Pallas kernels, all_steps(): pl.pallas_call(near_kernel, out_shape=jax.ShapeDtypeStruct((L, M, RHS), f...  41 us
    all_to_all x1, starting transfers between devices, all_steps(): parts = lax.all_to_all(partial, LEAF, 0, 0, tiled=True)  9.23 us
    pallas_call x1, Pallas kernels, all_steps(): pl.pallas_call(couple_kernel, out_shape=jax.ShapeDtypeStruct((NBASE, K, R...  8.41 us
    pallas_call x1, Pallas kernels, all_steps(): pl.pallas_call(up_kernel, out_shape=(jax.ShapeDtypeStruct((CHIPS, MSG, RH...  7.66 us
    unnamed x21, local copies, waits for them, and re-layouts  4.84 us
    pallas_call x1, Pallas kernels, all_steps(): pl.pallas_call(down_kernel, out_shape=jax.ShapeDtypeStruct((L, M, RHS), b...  4.09 us
    pallas_call x1, Pallas kernels, all_steps(): pl.pallas_call(early_kernel, out_shape=(jax.ShapeDtypeStruct((8, NBASE),...  3.81 us
  transfers between devices with their start and end apart: 4, of which 0 were waited for; matrix products, arithmetic and copies ran while one was open for 3% of the time, Pallas kernels for 41%

commit v1 on v0

--- a/solution.py
+++ b/solution.py
@@ -241,7 +241,7 @@
     def prepare(g, carry):
         points = coords[:, pl.ds(pl.multiple_of(g * M, M), M)]
         feats[g] = features(points, True).astype(bf16)
-        aims[g] = features(points, False).T.astype(bf16)
+        aims[g] = features(points, False).astype(bf16)
         return carry
 
     lax.fori_loop(0, LEAVES_DEV, prepare, 0, unroll=8)
@@ -249,7 +249,7 @@
 
 def near_kernel(
     columns, own_feats, own_aims, before, own, after, out,
-    pool, feats, aims, tails, points_s, kernel_a, kernel_b, sems,
+    pool, feats, aims, tails, points_s, kernel_a, kernel_b, done, sems,
 ):
     L = LEAVES_DEV
     tail_copies = [
@@ -287,24 +287,30 @@
         for j in range(0, NNEAR, 2):
             named = [columns[l * NNEAR + k] for k in range(j, min(j + 2, NNEAR))]
             theirs = jnp.concatenate([feats[g] for g in named], axis=1)
-            squares = jnp.dot(mine, theirs, preferred_element_type=f32)
+            squares = lax.dot_general(
+                mine, theirs, (((0,), (0,)), ((), ())), preferred_element_type=f32
+            )
             store[:, pl.ds(j * M, len(named) * M)] = lax.rsqrt(squares).astype(bf16)
 
     def apply(l, store):
         starts = [pl.multiple_of(columns[l * NNEAR + j] * M, M) for j in range(NNEAR)]
         named = jnp.concatenate([pool[pl.ds(start, M)] for start in starts], axis=0)
-        out[l] = jnp.dot(store[...], named, preferred_element_type=f32)
+        done[l] = jnp.dot(store[...], named, preferred_element_type=f32)
 
     weigh(0, kernel_a)
 
-    def two(i, carry):
-        weigh(2 * i + 1, kernel_b)
-        apply(2 * i, kernel_a)
-        weigh(jnp.minimum(2 * i + 2, L - 1), kernel_a)
-        apply(2 * i + 1, kernel_b)
+    def eight(i, carry):
+        for l in range(0, 8, 2):
+            weigh(8 * i + l + 1, kernel_b)
+            apply(8 * i + l, kernel_a)
+            weigh(jnp.minimum(8 * i + l + 2, L - 1), kernel_a)
+            apply(8 * i + l + 1, kernel_b)
+        part = pl.ds(8 * i, 8)
+        pltpu.make_async_copy(done.at[part], out.at[part], sems.at[7]).start()
         return carry
 
-    lax.fori_loop(0, L // 2, two, 0)
+    lax.fori_loop(0, L // 8, eight, 0)
+    pltpu.make_async_copy(done, out, sems.at[7]).wait()
 
 
 def down_kernel(parts, v_rows, near, out, parts_s, v_s, near_s, out_s, sems):
@@ -385,7 +391,7 @@
         out_shape=(
             jax.ShapeDtypeStruct((8, NBASE), jnp.int32),
             jax.ShapeDtypeStruct((L, FEAT, M), bf16),
-            jax.ShapeDtypeStruct((L, M, FEAT), bf16),
+            jax.ShapeDtypeStruct((L, FEAT, M), bf16),
         ),
         in_specs=[in_vmem()] * 2,
         out_specs=(in_vmem(),) * 3,
@@ -426,16 +432,17 @@
         near_kernel,
         out_shape=jax.ShapeDtypeStruct((L, M, RHS), f32),
         in_specs=[in_smem()] + [in_place()] * 5,
-        out_specs=in_vmem(),
+        out_specs=in_place(),
         scratch_shapes=[
             pltpu.VMEM((3 * POINTS, RHS), bf16),
             pltpu.VMEM((3 * L, FEAT, M), bf16),
-            pltpu.VMEM((L, M, FEAT), bf16),
+            pltpu.VMEM((L, FEAT, M), bf16),
             pltpu.VMEM((2, TAIL, M), bf16),
             pltpu.VMEM((2, 3 * L, M), f32),
             pltpu.VMEM((M, NNEAR * M), bf16),
             pltpu.VMEM((M, NNEAR * M), bf16),
-            pltpu.SemaphoreType.DMA((7,)),
+            pltpu.VMEM((L, M, RHS), f32),
+            pltpu.SemaphoreType.DMA((8,)),
         ],
         name="near",
         cost_estimate=pl.CostEstimate(

time: 129 us -> 124 us (0.961)
  Pallas kernels: 64.9 us -> 59.4 us
    pallas_call x1, Pallas kernels: 41 us -> 36.5 us  [all_steps(): pl.pallas_call(near_kernel, out_shape=jax.ShapeDtypeStruct((L, M, RHS), f...]
  transfers between devices with their start and end apart: 4 -> 4, of which waited for: 0 -> 0; matrix products, arithmetic and copies ran while one was open for 3% -> 3% of each run, Pallas kernels for 41% -> 39%
where the time goes in v1:
time: 124 us; the launch traced here: 123 us
  Pallas kernels  59.4 us (48%)
  blocking collectives  45.3 us (37%)
  starting transfers between devices  12 us (10%)
  local copies, waits for them, and re-layouts  6.17 us (5%)
    all_to_all x1, blocking collectives, all_steps(): mine = lax.all_to_all(message, LEAF[:3], 0, 0, tiled=True)  45.3 us
    pallas_call x1, Pallas kernels, all_steps(): pl.pallas_call(near_kernel, out_shape=jax.ShapeDtypeStruct((L, M, RHS), f...  36.5 us
    all_to_all x1, starting transfers between devices, all_steps(): parts = lax.all_to_all(partial, LEAF, 0, 0, tiled=True)  9.23 us
    pallas_call x1, Pallas kernels, all_steps(): pl.pallas_call(couple_kernel, out_shape=jax.ShapeDtypeStruct((NBASE, K, R...  8.35 us
    pallas_call x1, Pallas kernels, all_steps(): pl.pallas_call(up_kernel, out_shape=(jax.ShapeDtypeStruct((CHIPS, MSG, RH...  7.69 us
    unnamed x21, local copies, waits for them, and re-layouts  4.84 us
    pallas_call x1, Pallas kernels, all_steps(): pl.pallas_call(down_kernel, out_shape=jax.ShapeDtypeStruct((L, M, RHS), b...  4.09 us
    pallas_call x1, Pallas kernels, all_steps(): pl.pallas_call(early_kernel, out_shape=(jax.ShapeDtypeStruct((8, NBASE),...  2.77 us
  transfers between devices with their start and end apart: 4, of which 0 were waited for; matrix products, arithmetic and copies ran while one was open for 3% of the time, Pallas kernels for 39%

profile of v1, /device:TPU:0, one launch (start us, length us, event | category | flops | bytes accessed | tf_op | source)
XLA Modules:
  0.0 123.0 jit_solution(4636800867320819725)
XLA Ops:
  0.0 0.0 copy-start.5
  0.0 0.0 copy-start.3
  0.0 0.0 copy-start.2
  0.0 7.7 %up.1 = (bf16[64,48,128]{2,1,0:T(8,128)(2,1)}, bf16[16,128,128]{2,1,0:T(8,128)(2,1)}, bf16[8768,128]{1,0:T(8,128)(2,1)}) custom-call(bf16[8192,128]{1,0:T(8,128)(2,1)} %own.1, f32[3,8192]{1,0:T(4,128)} %coords.3, bf16[64,4096]{1,0:T(8,128)(2,1)} %basis.1, bf16[64,1024]{1,0:T(8,128)(2,1)} %leaf_rows.1, bf16[8,1024]{1,0:T(8,128)(2,1)} %mid_rows.1, ...), custom_call_target="tpu_custom_call" | custom-call | flops 2000000000 | bytes 5000000 | tf_op jit(solution)/shard_map/up/pallas_call | solution.py:363
  7.7 0.0 copy-start.4
  7.7 0.0 copy-start.6
  7.7 1.4 %collective-permute-start.1 = (bf16[8768,128]{1,0:T(8,128)(2,1)}, bf16[8768,128]{1,0:T(8,128)(2,1)S(1)}, u32[]{:S(2)}, u32[]{:S(2)}) collective-permute-start(bf16[8768,128]{1,0:T(8,128)(2,1)} %get-tuple-element.16), channel_id=1, source_target_pairs={{0,1},{1,2},{2,3},{3,4},{4,5},{5,6},{6,7},{7,8},{8,9},{9,10},{10,1... | collective-permute-start | bytes 6733832 | tf_op jit(solution)/shard_map/ppermute | solution.py:386
  9.2 1.3 %collective-permute-start.2 = (bf16[8768,128]{1,0:T(8,128)(2,1)}, bf16[8768,128]{1,0:T(8,128)(2,1)}, u32[]{:S(2)}, u32[]{:S(2)}) collective-permute-start(bf16[8768,128]{1,0:T(8,128)(2,1)} %get-tuple-element.16), channel_id=1, source_target_pairs={{1,0},{2,1},{3,2},{4,3},{5,4},{6,5},{7,6},{8,7},{9,8},{10,9},{11,1... | collective-permute-start | bytes 6733832 | tf_op jit(solution)/shard_map/ppermute | solution.py:387
  10.5 45.3 %all_to_all.10.mine = bf16[64,48,128]{2,1,0:T(8,128)(2,1)S(1)} all-to-all(bf16[64,48,128]{2,1,0:T(8,128)(2,1)} %get-tuple-element.12), channel_id=1, replica_groups=mesh['leaf_0'=4,'leaf_1'=4,'leaf_2'=4,'leaf_3'=2] {'leaf_0','leaf_1','le..., dimensions={0} | all-to-all | bytes 1572864 | tf_op jit(solution)/shard_map/all_to_all | solution.py:384
  55.8 0.0 copy-start.1
  55.8 0.0 collective-permute-start
  55.8 0.0 copy-done.5
  55.8 0.9 copy.15.base_target
  56.7 0.0 copy-done.3
  56.7 0.1 copy.16
  56.8 0.7 reshape.18.columns
  57.5 0.0 copy-done.2
  57.6 0.8 copy.17
  58.4 0.0 copy-done.4
  58.4 0.6 copy.20
  59.0 0.0 copy-done.6
  59.0 0.6 pad.8.sources
  59.6 2.8 %early.1 = (s32[8,128]{1,0:T(8,128)}, bf16[64,48,128]{2,1,0:T(8,128)(2,1)}, bf16[64,48,128]{2,1,0:T(8,128)(2,1)}) custom-call(s32[189,1]{1,0:T(8,128)} %copy.15.base_target, f32[3,8192]{1,0:T(4,128)} %coords.3), custom_call_target="tpu_custom_call" | custom-call | flops 1000000000 | bytes 1000000 | tf_op jit(solution)/shard_map/early/pallas_call | solution.py:389
  62.4 0.0 copy-done.1
  62.4 0.0 collective-permute-done.other
  62.4 8.4 %couple.1 = bf16[128,32,128]{2,1,0:T(8,128)(2,1)} custom-call(s32[1]{0:T(128)} %bitcast.core, s32[8,128]{1,0:T(8,128)} %get-tuple-element.11.table, s32[192]{0:T(256)} %pad.8.sources, s32[8]{0:T(128)} %top_target.1, s32[8]{0:T(128)} %top_source.1, bf16[64,48,128]{2,1,0:T(8,128)(2,1)} %copy-done.1, bf16[64,48,128]{2,1,0:T(8,128)(2,1)} %collective-permute-done.other, ...), custom_call_target="tpu_custom_call" | custom-call | flops 2000000000 | bytes 5000000 | tf_op jit(solution)/shard_map/couple/pallas_call | solution.py:405
  70.7 9.2 %all-to-all-start.1 = ((bf16[128,32,128]{2,1,0:T(8,128)(2,1)}), bf16[128,32,128]{2,1,0:T(8,128)(2,1)S(1)}, u32[]{:S(2)}, u32[]{:S(2)}) async-start(bf16[128,32,128]{2,1,0:T(8,128)(2,1)} %couple.1), calls=%async_computation.1 | async-start | bytes 2097152 | tf_op jit(solution)/shard_map/all_to_all | solution.py:429
  80.0 0.0 collective-permute-done.1.before
  80.0 0.0 copy-start.7
  80.0 0.0 collective-permute-done.2.after
  80.0 1.4 %copy-done.7 = bf16[8768,128]{1,0:T(8,128)(2,1)} copy-done((bf16[8768,128]{1,0:T(8,128)(2,1)}, bf16[8768,128]{1,0:T(8,128)(2,1)S(1)}, u32[]{:S(2)}) %copy-start.7) | copy-done | bytes 2244632
  81.4 36.5 %near.1 = f32[64,128,128]{2,1,0:T(8,128)} custom-call(s32[1728]{0:T(1024)} %reshape.18.columns, bf16[64,48,128]{2,1,0:T(8,128)(2,1)} %get-tuple-element.14.own_feats, bf16[64,48,128]{2,1,0:T(8,128)(2,1)} %get-tuple-element.15.own_aims, bf16[8768,128]{1,0:T(8,128)(2,1)} %copy-done.7, bf16[8192,128]{1,0:T(8,128)(2,1)} %own.1, ...), custom_call_target="tpu_custom_call" | custom-call | flops 40000000000 | bytes 10000000 | tf_op jit(solution)/shard_map/near/pallas_call | solution.py:431
  117.9 0.0 all-to-all-done.1.parts
  117.9 0.0 copy-start
  117.9 1.0 copy-done
  118.9 4.1 %down.1 = bf16[64,128,128]{2,1,0:T(8,128)(2,1)} custom-call(bf16[128,32,128]{2,1,0:T(8,128)(2,1)} %copy-done, bf16[16,128,128]{2,1,0:T(8,128)(2,1)} %get-tuple-element.13.v_rows, f32[64,128,128]{2,1,0:T(8,128)} %near.1), custom_call_target="tpu_custom_call" | custom-call | flops 1000000000 | bytes 10000000 | tf_op jit(solution)/shard_map/down/pallas_call | solution.py:453
  (1 shorter events, 0.0 us)
Async XLA Ops:
  0.0 55.8 %copy-start.5 = (s32[189,1]{0,1:T(1,128)S(1)}, s32[189,1]{0,1:T(1,128)}, u32[]{:S(2)}) copy-start(s32[189,1]{0,1:T(1,128)} %param.21) | copy-start | bytes 2272
  0.0 56.7 %copy-start.3 = (s32[64,27]{0,1:T(8,128)S(1)}, s32[64,27]{0,1:T(8,128)}, u32[]{:S(2)}) copy-start(s32[64,27]{0,1:T(8,128)} %param.15) | copy-start | bytes 20740
  0.0 57.5 %copy-start.2 = (bf16[189,1024]{1,0:T(8,128)(2,1)S(1)}, bf16[189,1024]{1,0:T(8,128)(2,1)}, u32[]{:S(2)}) copy-start(bf16[189,1024]{1,0:T(8,128)(2,1)} %param.20) | copy-start | bytes 1161220
  7.7 50.7 %copy-start.4 = (bf16[8,1024]{1,0:T(8,128)(2,1)S(1)}, bf16[8,1024]{1,0:T(8,128)(2,1)}, u32[]{:S(2)}) copy-start(bf16[8,1024]{1,0:T(8,128)(2,1)} %param.23) | copy-start | bytes 49156
  7.7 51.3 %copy-start.6 = (s32[189]{0:T(256)S(1)}, s32[189]{0:T(256)}, u32[]{:S(2)}) copy-start(s32[189]{0:T(256)} %param.22) | copy-start | bytes 2272
  7.7 72.2 %collective-permute-start.1 = (bf16[8768,128]{1,0:T(8,128)(2,1)}, bf16[8768,128]{1,0:T(8,128)(2,1)S(1)}, u32[]{:S(2)}, u32[]{:S(2)}) collective-permute-start(bf16[8768,128]{1,0:T(8,128)(2,1)} %get-tuple-element.16), channel_id=1, source_target_pairs={{0,1},{1,2},{2,3},{3,4},{4,5},{5,6},{6,7},{7,8},{8,9},{9,10},{10,1... | collective-permute-start | bytes 6733832 | tf_op jit(solution)/shard_map/ppermute | solution.py:386
  9.2 70.8 %collective-permute-start.2 = (bf16[8768,128]{1,0:T(8,128)(2,1)}, bf16[8768,128]{1,0:T(8,128)(2,1)}, u32[]{:S(2)}, u32[]{:S(2)}) collective-permute-start(bf16[8768,128]{1,0:T(8,128)(2,1)} %get-tuple-element.16), channel_id=1, source_target_pairs={{1,0},{2,1},{3,2},{4,3},{5,4},{6,5},{7,6},{8,7},{9,8},{10,9},{11,1... | collective-permute-start | bytes 6733832 | tf_op jit(solution)/shard_map/ppermute | solution.py:387
  55.8 6.6 %copy-start.1 = (bf16[64,48,128]{2,1,0:T(8,128)(2,1)}, bf16[64,48,128]{2,1,0:T(8,128)(2,1)S(1)}, u32[]{:S(2)}) copy-start(bf16[64,48,128]{2,1,0:T(8,128)(2,1)S(1)} %all_to_all.10.mine) | copy-start | bytes 2359300
  55.8 6.6 %collective-permute-start = (bf16[64,48,128]{2,1,0:T(8,128)(2,1)S(1)}, bf16[64,48,128]{2,1,0:T(8,128)(2,1)}, u32[]{:S(2)}, u32[]{:S(2)}) collective-permute-start(bf16[64,48,128]{2,1,0:T(8,128)(2,1)S(1)} %all_to_all.10.mine), channel_id=1, source_target_pairs={{0,1},{1,0},{2,3},{3,2},{4,5},{5,4},{6,7},{7,6},{8,9},{9,8},{10,11... | collective-permute-start | bytes 2359304 | tf_op jit(solution)/shard_map/ppermute | solution.py:385
  70.7 47.2 %all-to-all-start.1 = ((bf16[128,32,128]{2,1,0:T(8,128)(2,1)}), bf16[128,32,128]{2,1,0:T(8,128)(2,1)S(1)}, u32[]{:S(2)}, u32[]{:S(2)}) async-start(bf16[128,32,128]{2,1,0:T(8,128)(2,1)} %couple.1), calls=%async_computation.1 | async-start | bytes 2097152 | tf_op jit(solution)/shard_map/all_to_all | solution.py:429
  80.0 1.4 %copy-start.7 = (bf16[8768,128]{1,0:T(8,128)(2,1)}, bf16[8768,128]{1,0:T(8,128)(2,1)S(1)}, u32[]{:S(2)}) copy-start(bf16[8768,128]{1,0:T(8,128)(2,1)S(1)} %collective-permute-done.1.before) | copy-start | bytes 6733828
  117.9 1.0 copy-start

commit v2 on v1

--- a/solution.py
+++ b/solution.py
@@ -18,9 +18,12 @@
 CHIPS = 64
 NTOP = 16
 BLK_DEV = 189
-BLK_PAD = 192
 TOPB_DEV = 8
 FEAT = 48
+OWN = 6
+REST = NNEAR - OWN
+UNITS = 8
+SPARE = 40
 POINTS = 8192
 TAIL = 576
 MSG = 48
@@ -133,8 +136,8 @@
 
 
 def couple_kernel(
-    core, table, sources, top_target, top_source, mine, other, tiles, top_tiles, out,
-    gathered, top_sum, top_rows, sems,
+    core, table, sources, top_target, top_source, mine, other, block_rows, top_block_rows, out,
+    gathered, top_sum, top_rows, tiles_s, top_s, sems,
 ):
     me = core[0]
     copies = [
@@ -143,8 +146,16 @@
     ]
     for copy in copies:
         copy.start()
+    for i in range(8):
+        piece = pl.ds(i * 128, 128)
+        top_s[pl.ds(i, TOPB_DEV, stride=8), :] = top_block_rows[:, piece].astype(f32)
+        for b in range(0, BLK_DEV, 8):
+            n = min(8, BLK_DEV - b)
+            tiles_s[pl.ds(8 * b + i, n, stride=8), :] = block_rows[pl.ds(b, n), piece].astype(f32)
+    tiles_s[pl.ds(8 * BLK_DEV, 8), :] = jnp.zeros((8, 128), f32)
     for copy in copies:
         copy.wait()
+
     top_sum[...] = jnp.zeros((NTOP, K, RHS), f32)
     lifted = []
     for b in range(TOPB_DEV):
@@ -163,7 +174,7 @@
         )
     products = [
         jnp.dot(
-            stacked_groups(top_tiles[b]).astype(bf16),
+            stacked_groups(top_s[pl.ds(8 * b, 8), :]).astype(bf16),
             four_times(lifted[b]),
             preferred_element_type=f32,
         )
@@ -181,8 +192,8 @@
         lhs, rhs = [], []
         for row in (0, 1):
             b = table[row, d]
-            s = sources[b]
-            lhs.append(stacked_groups(tiles[b]))
+            s = sources[jnp.minimum(b, BLK_DEV - 1)]
+            lhs.append(stacked_groups(tiles_s[pl.ds(pl.multiple_of(8 * b, 8), 8), :]))
             rhs.append(four_times(gathered[(s % 2) * CHIPS + s // 2, :K]))
         lhs.append(stacked_groups(gathered[(d % 2) * CHIPS + d // 2, 32:40]))
         rhs.append(four_times(top_rows[d // 8]))
@@ -228,15 +239,54 @@
     return jnp.concatenate(done, axis=0)
 
 
-def early_kernel(base_target, coords, table, feats, aims):
-    targets = base_target[...]
-    block = lax.broadcasted_iota(jnp.int32, (BLK_DEV, NBASE), 0)
-    here = targets == lax.broadcasted_iota(jnp.int32, (BLK_DEV, NBASE), 1)
-    first = jnp.min(jnp.where(here, block, BLK_DEV), axis=0, keepdims=True)
-    last = jnp.max(jnp.where(here, block, -1), axis=0, keepdims=True)
-    table[...] = jnp.zeros((8, NBASE), jnp.int32)
-    table[0:1] = first
-    table[1:2] = jnp.where(last > first, last, BLK_DEV)
+def early_kernel(near_leaves, base_target, coords, columns, table, feats, aims, named_s):
+    L = LEAVES_DEV
+    named_s[:, pl.ds(0, NNEAR)] = near_leaves[...]
+    named = named_s[...]
+    lane = lax.broadcasted_iota(jnp.int32, (L, 128), 1)
+    valid = lane < NNEAR
+    own = valid & (named >= L) & (named < 2 * L)
+    earlier = lax.broadcasted_iota(jnp.int32, (128, 128), 0) < lax.broadcasted_iota(jnp.int32, (128, 128), 1)
+    rank = jnp.dot(
+        jnp.where(own, 1.0, 0.0).astype(bf16),
+        jnp.where(earlier, 1.0, 0.0).astype(bf16),
+        preferred_element_type=f32,
+    ).astype(jnp.int32)
+    count = jnp.sum(jnp.where(own, 1, 0), axis=1, keepdims=True)
+    taken = own & (rank < OWN)
+    place = jnp.where(taken, rank, OWN + lane - jnp.minimum(rank, OWN))
+    place = jnp.where(valid, place, -1)
+    value = jnp.where(taken, named - L, named)
+    ordered = jnp.where(lane < OWN, L, 3 * L)
+    for j in range(NNEAR):
+        ordered = jnp.where(lane == place[:, j : j + 1], value[:, j : j + 1], ordered)
+    columns[...] = ordered
+
+    pairs = (OWN - jnp.minimum(count, OWN) + 1) // 2
+    wide = jnp.broadcast_to(pairs, (L, 128))
+    upto = lax.broadcasted_iota(jnp.int32, (L, L), 1) <= lax.broadcasted_iota(jnp.int32, (L, L), 0)
+    ends = jnp.dot(
+        jnp.where(upto, 1.0, 0.0).astype(bf16), wide.astype(f32).astype(bf16), preferred_element_type=f32
+    ).astype(jnp.int32)
+    total = jnp.sum(wide, axis=0, keepdims=True)
+    table[...] = jnp.zeros((8, 256), jnp.int32)
+    for block in range(2):
+        unit = lane + 128 * block
+        passed = ends <= unit
+        leaf = jnp.sum(jnp.where(passed, 1, 0), axis=0, keepdims=True)
+        slot = unit[:1] - jnp.sum(jnp.where(passed, wide, 0), axis=0, keepdims=True)
+        code = jnp.where(unit[:1] < total, leaf * 64 + NNEAR + 2 * slot, SPARE)
+        table[2:3, pl.ds(128 * block, 128)] = code
+    table[3:4, pl.ds(0, 128)] = total
+
+    block = lax.broadcasted_iota(jnp.int32, (NBASE, BLK_DEV), 1)
+    here = base_target[...] == lax.broadcasted_iota(jnp.int32, (NBASE, BLK_DEV), 0)
+    first = jnp.min(jnp.where(here, block, BLK_DEV), axis=1, keepdims=True)
+    last = jnp.max(jnp.where(here, block, -1), axis=1, keepdims=True)
+    second = jnp.where(last > first, last, BLK_DEV)
+    for row, slot in enumerate((first, second)):
+        turned = jnp.broadcast_to(slot.astype(f32), (NBASE, 128)).T
+        table[row : row + 1, pl.ds(0, 128)] = turned[0:1].astype(jnp.int32)
 
     def prepare(g, carry):
         points = coords[:, pl.ds(pl.multiple_of(g * M, M), M)]
@@ -247,45 +297,13 @@
     lax.fori_loop(0, LEAVES_DEV, prepare, 0, unroll=8)
 
 
-def near_kernel(
-    columns, own_feats, own_aims, before, own, after, out,
-    pool, feats, aims, tails, points_s, kernel_a, kernel_b, done, sems,
-):
+def near_leaves_loop(first, number, columns, feats, aims, pool, done, out, kernel_a, kernel_b, sem, add):
     L = LEAVES_DEV
-    tail_copies = [
-        pltpu.make_async_copy(part.at[pl.ds(POINTS, TAIL)], tails.at[i], sems.at[i])
-        for i, part in enumerate((before, after))
-    ]
-    copies = [
-        pltpu.make_async_copy(own_aims, aims, sems.at[2]),
-        pltpu.make_async_copy(own_feats, feats.at[pl.ds(L, L)], sems.at[3]),
-    ]
-    copies += [
-        pltpu.make_async_copy(
-            part.at[pl.ds(0, POINTS)], pool.at[pl.ds(i * POINTS, POINTS)], sems.at[4 + i]
-        )
-        for i, part in enumerate((before, own, after))
-    ]
-    for copy in tail_copies + copies:
-        copy.start()
-    for i in range(2):
-        tail_copies[i].wait()
-        part = [tails[i, pl.ds(p * 3 * L, 3 * L)].astype(f32) for p in range(3)]
-        points_s[i] = part[0] + part[1] + part[2]
-
-        def prepare(g, carry, i=i):
-            points = points_s[i, pl.ds(g, 3, stride=L), :]
-            feats[2 * i * L + g] = features(points, True).astype(bf16)
-            return carry
-
-        lax.fori_loop(0, L, prepare, 0, unroll=8)
-    for copy in copies:
-        copy.wait()
 
     def weigh(l, store):
         mine = aims[l]
-        for j in range(0, NNEAR, 2):
-            named = [columns[l * NNEAR + k] for k in range(j, min(j + 2, NNEAR))]
+        for j in range(0, number, 2):
+            named = [columns[l, first + k] for k in range(j, min(j + 2, number))]
             theirs = jnp.concatenate([feats[g] for g in named], axis=1)
             squares = lax.dot_general(
                 mine, theirs, (((0,), (0,)), ((), ())), preferred_element_type=f32
@@ -293,9 +311,10 @@
             store[:, pl.ds(j * M, len(named) * M)] = lax.rsqrt(squares).astype(bf16)
 
     def apply(l, store):
-        starts = [pl.multiple_of(columns[l * NNEAR + j] * M, M) for j in range(NNEAR)]
+        starts = [pl.multiple_of(columns[l, first + j] * M, M) for j in range(number)]
         named = jnp.concatenate([pool[pl.ds(start, M)] for start in starts], axis=0)
-        done[l] = jnp.dot(store[...], named, preferred_element_type=f32)
+        field = jnp.dot(store[...], named, preferred_element_type=f32)
+        done[l] = done[l] + field if add else field
 
     weigh(0, kernel_a)
 
@@ -306,18 +325,135 @@
             weigh(jnp.minimum(8 * i + l + 2, L - 1), kernel_a)
             apply(8 * i + l + 1, kernel_b)
         part = pl.ds(8 * i, 8)
-        pltpu.make_async_copy(done.at[part], out.at[part], sems.at[7]).start()
+        pltpu.make_async_copy(done.at[part], out.at[part], sem).start()
         return carry
 
     lax.fori_loop(0, L // 8, eight, 0)
-    pltpu.make_async_copy(done, out, sems.at[7]).wait()
-
-
-def down_kernel(parts, v_rows, near, out, parts_s, v_s, near_s, out_s, sems):
+    pltpu.make_async_copy(done, out, sem).wait()
+
+
+def own_kernel(columns, own_feats, own_aims, charges, out, pool, feats, aims, kernel_a, kernel_b, done, sems):
+    L = LEAVES_DEV
+    copies = [
+        pltpu.make_async_copy(own_aims, aims, sems.at[0]),
+        pltpu.make_async_copy(own_feats, feats.at[pl.ds(0, L)], sems.at[1]),
+        pltpu.make_async_copy(charges, pool.at[pl.ds(0, POINTS)], sems.at[2]),
+    ]
+    for copy in copies:
+        copy.start()
+    pool[pl.ds(POINTS, M)] = jnp.zeros((M, RHS), bf16)
+    for copy in copies:
+        copy.wait()
+    feats[L] = feats[0]
+
+    def weigh(batch, store):
+        for u in range(8):
+            l = jnp.minimum(8 * batch + u, L - 1)
+            for j in range(0, OWN, 2):
+                theirs = jnp.concatenate([feats[columns[l, j]], feats[columns[l, j + 1]]], axis=1)
+                squares = lax.dot_general(
+                    aims[l], theirs, (((0,), (0,)), ((), ())), preferred_element_type=f32
+                )
+                store[u, :, pl.ds(j * M, 2 * M)] = lax.rsqrt(squares).astype(bf16)
+
+    def apply(batch, store):
+        for u in range(8):
+            l = 8 * batch + u
+            starts = [pl.multiple_of(columns[l, j] * M, M) for j in range(OWN)]
+            named = jnp.concatenate([pool[pl.ds(start, M)] for start in starts], axis=0)
+            done[l] = jnp.dot(store[u], named, preferred_element_type=f32)
+        part = pl.ds(8 * batch, 8)
+        pltpu.make_async_copy(done.at[part], out.at[part], sems.at[3]).start()
+
+    weigh(0, kernel_a)
+
+    def two(i, carry):
+        weigh(2 * i + 1, kernel_b)
+        apply(2 * i, kernel_a)
+        weigh(2 * i + 2, kernel_a)
+        apply(2 * i + 1, kernel_b)
+        return carry
+
+    lax.fori_loop(0, L // 16, two, 0)
+    pltpu.make_async_copy(done, out, sems.at[3]).wait()
+
+
+def near_kernel(
+    columns, table, own_feats, own_aims, before, own, after, so_far, out,
+    pool, feats, aims, tails, points_s, kernel_a, kernel_b, units_a, units_b, done, sems,
+):
+    L = LEAVES_DEV
+    tail_copies = [
+        pltpu.make_async_copy(part.at[pl.ds(POINTS, TAIL)], tails.at[i], sems.at[i])
+        for i, part in enumerate((before, after))
+    ]
+    copies = [
+        pltpu.make_async_copy(own_aims, aims, sems.at[2]),
+        pltpu.make_async_copy(own_feats, feats.at[pl.ds(L, L)], sems.at[3]),
+    ]
+    copies += [
+        pltpu.make_async_copy(
+            part.at[pl.ds(0, POINTS)], pool.at[pl.ds(i * POINTS, POINTS)], sems.at[4 + i]
+        )
+        for i, part in enumerate((before, own, after))
+    ]
+    copies.append(pltpu.make_async_copy(so_far, done, sems.at[7]))
+    for copy in tail_copies + copies:
+        copy.start()
+    pool[pl.ds(3 * POINTS, M)] = jnp.zeros((M, RHS), bf16)
+    for i in range(2):
+        tail_copies[i].wait()
+        part = [tails[i, pl.ds(p * 3 * L, 3 * L)].astype(f32) for p in range(3)]
+        points_s[i] = part[0] + part[1] + part[2]
+
+        def prepare(g, carry, i=i):
+            points = points_s[i, pl.ds(g, 3, stride=L), :]
+            feats[2 * i * L + g] = features(points, True).astype(bf16)
+            return carry
+
+        lax.fori_loop(0, L, prepare, 0, unroll=8)
+    feats[3 * L] = feats[0]
+    for copy in copies:
+        copy.wait()
+
+    def unit(v):
+        code = table[2, v]
+        leaf, slot = code // 64, code % 64
+        return leaf, columns[leaf, slot], columns[leaf, slot + 1]
+
+    def weigh(batch, store):
+        for u in range(UNITS):
+            leaf, g, h = unit(batch * UNITS + u)
+            theirs = jnp.concatenate([feats[g], feats[h]], axis=1)
+            squares = lax.dot_general(
+                aims[leaf], theirs, (((0,), (0,)), ((), ())), preferred_element_type=f32
+            )
+            store[u] = lax.rsqrt(squares).astype(bf16)
+
+    def apply(batch, store):
+        for u in range(UNITS):
+            leaf, g, h = unit(batch * UNITS + u)
+            starts = [pl.multiple_of(k * M, M) for k in (g, h)]
+            named = jnp.concatenate([pool[pl.ds(start, M)] for start in starts], axis=0)
+            done[leaf] = done[leaf] + jnp.dot(store[u], named, preferred_element_type=f32)
+
+    def two(i, carry):
+        weigh(2 * i, units_a)
+        weigh(2 * i + 1, units_b)
+        apply(2 * i, units_a)
+        apply(2 * i + 1, units_b)
+        return carry
+
+    lax.fori_loop(0, (table[3, 0] + 2 * UNITS - 1) // (2 * UNITS), two, 0)
+    near_leaves_loop(
+        OWN, REST, columns, feats, aims, pool, done, out, kernel_a, kernel_b, sems.at[8], True
+    )
+
+
+def down_kernel(parts, v_rows, near, out, v_s, near_s, out_s, sems):
     steps = LEAVES_DEV // 8
     chunks = [pl.ds(8 * i, 8) for i in range(steps)]
     first = [
-        pltpu.make_async_copy(parts, parts_s, sems.at[0]),
         pltpu.make_async_copy(v_rows, v_s, sems.at[1]),
     ]
     loads = [
@@ -329,14 +465,13 @@
     to = lax.broadcasted_iota(jnp.int32, (K, NBASE * K), 0)
     at = lax.broadcasted_iota(jnp.int32, (K, NBASE * K), 1) % K
     order = jnp.where(to == 4 * (at % 8) + at // 8, 1.0, 0.0).astype(bf16)
-    first[0].wait()
-    field = jnp.dot(order, parts_s[...].reshape(NBASE * K, RHS), preferred_element_type=f32)
+    field = jnp.dot(order, parts[...].reshape(NBASE * K, RHS), preferred_element_type=f32)
     zero = jnp.zeros((K, RHS), f32)
     spread = [
         jnp.concatenate([field if g == h else zero for h in range(4)], axis=0) for g in range(4)
     ]
     spread = jnp.concatenate(spread, axis=1).astype(bf16)
-    first[1].wait()
+    first[0].wait()
     stores = []
     for i, chunk in enumerate(chunks):
         rows = v_s[pl.ds(2 * i, 2)].reshape(2 * M, 4 * K)
@@ -386,31 +521,38 @@
     before = lax.ppermute(halo, LEAF, up)
     after = lax.ppermute(halo, LEAF, down)
 
-    table, own_feats, own_aims = pl.pallas_call(
+    columns, table, own_feats, own_aims = pl.pallas_call(
         early_kernel,
         out_shape=(
-            jax.ShapeDtypeStruct((8, NBASE), jnp.int32),
+            jax.ShapeDtypeStruct((L, 128), jnp.int32),
+            jax.ShapeDtypeStruct((8, 256), jnp.int32),
             jax.ShapeDtypeStruct((L, FEAT, M), bf16),
             jax.ShapeDtypeStruct((L, FEAT, M), bf16),
         ),
-        in_specs=[in_vmem()] * 2,
-        out_specs=(in_vmem(),) * 3,
+        in_specs=[in_vmem()] * 3,
+        out_specs=(in_vmem(),) * 4,
+        scratch_shapes=[pltpu.VMEM((L, 128), jnp.int32)],
         name="early",
         cost_estimate=pl.CostEstimate(flops=10**9, bytes_accessed=10**6, transcendentals=0),
-    )(base_target, coords)
-
-    spare = BLK_PAD - BLK_DEV
-    tiles = jnp.pad(base_coupling, ((0, spare), (0, 0))).reshape(BLK_PAD, 8, 128)
-    sources = jnp.pad(base_source, (0, spare))
+    )(
+        near_leaves,
+        base_target.reshape(1, BLK_DEV),
+        coords,
+    )
+
+    mine = pltpu.with_memory_space_constraint(mine, pltpu.VMEM)
+    other = pltpu.with_memory_space_constraint(other, pltpu.VMEM)
     partial = pl.pallas_call(
         couple_kernel,
         out_shape=jax.ShapeDtypeStruct((NBASE, K, RHS), bf16),
-        in_specs=[in_smem()] * 5 + [in_place()] * 2 + [in_vmem()] * 2,
+        in_specs=[in_smem()] * 5 + [in_vmem()] * 4,
         out_specs=in_vmem(),
         scratch_shapes=[
             pltpu.VMEM((NBASE, MSG, RHS), bf16),
             pltpu.VMEM((NTOP, K, RHS), f32),
             pltpu.VMEM((NTOP, K, RHS), bf16),
+            pltpu.VMEM((8 * BLK_DEV + 8, 128), f32),
+            pltpu.VMEM((8 * TOPB_DEV, 128), f32),
             pltpu.SemaphoreType.DMA((2,)),
         ],
         name="couple",
@@ -418,45 +560,65 @@
     )(
         lax.axis_index(LEAF[3]).reshape(1).astype(jnp.int32),
         table,
-        sources,
+        base_source,
         top_target,
         top_source,
         mine,
         other,
-        tiles,
-        top_coupling.reshape(TOPB_DEV, 8, 128),
+        base_coupling,
+        top_coupling,
     )
     parts = lax.all_to_all(partial, LEAF, 0, 0, tiled=True)
 
+    near_own = pl.pallas_call(
+        own_kernel,
+        out_shape=jax.ShapeDtypeStruct((L, M, RHS), f32),
+        in_specs=[in_smem()] + [in_place()] * 3,
+        out_specs=in_place(),
+        scratch_shapes=[
+            pltpu.VMEM((POINTS + M, RHS), bf16),
+            pltpu.VMEM((L + 1, FEAT, M), bf16),
+            pltpu.VMEM((L, FEAT, M), bf16),
+            pltpu.VMEM((8, M, OWN * M), bf16),
+            pltpu.VMEM((8, M, OWN * M), bf16),
+            pltpu.VMEM((L, M, RHS), f32),
+            pltpu.SemaphoreType.DMA((4,)),
+        ],
+        name="own",
+        cost_estimate=pl.CostEstimate(
+            flops=10**10, bytes_accessed=10**7, transcendentals=7 * 10**6
+        ),
+    )(columns, own_feats, own_aims, charges)
     near = pl.pallas_call(
         near_kernel,
         out_shape=jax.ShapeDtypeStruct((L, M, RHS), f32),
-        in_specs=[in_smem()] + [in_place()] * 5,
+        in_specs=[in_smem()] * 2 + [in_place()] * 6,
         out_specs=in_place(),
         scratch_shapes=[
-            pltpu.VMEM((3 * POINTS, RHS), bf16),
-            pltpu.VMEM((3 * L, FEAT, M), bf16),
+            pltpu.VMEM((3 * POINTS + M, RHS), bf16),
+            pltpu.VMEM((3 * L + 1, FEAT, M), bf16),
             pltpu.VMEM((L, FEAT, M), bf16),
             pltpu.VMEM((2, TAIL, M), bf16),
             pltpu.VMEM((2, 3 * L, M), f32),
-            pltpu.VMEM((M, NNEAR * M), bf16),
-            pltpu.VMEM((M, NNEAR * M), bf16),
+            pltpu.VMEM((M, REST * M), bf16),
+            pltpu.VMEM((M, REST * M), bf16),
+            pltpu.VMEM((UNITS, M, 2 * M), bf16),
+            pltpu.VMEM((UNITS, M, 2 * M), bf16),
             pltpu.VMEM((L, M, RHS), f32),
-            pltpu.SemaphoreType.DMA((8,)),
+            pltpu.SemaphoreType.DMA((9,)),
         ],
         name="near",
         cost_estimate=pl.CostEstimate(
             flops=4 * 10**10, bytes_accessed=10**7, transcendentals=3 * 10**7
         ),
-    )(near_leaves.reshape(-1), own_feats, own_aims, before, charges, after)
+    )(columns, table, own_feats, own_aims, before, charges, after, near_own)
 
     potential = pl.pallas_call(
         down_kernel,
         out_shape=jax.ShapeDtypeStruct((L, M, RHS), bf16),
-        in_specs=[in_place()] * 3,
+        in_specs=[in_vmem()] + [in_place()] * 2,
         out_specs=in_place(),
         scratch_shapes=[
-            pltpu.VMEM((NBASE, K, RHS), bf16),
             pltpu.VMEM((L // 4, M, 4 * K), bf16),
             pltpu.VMEM((L, M, RHS), f32),
             pltpu.VMEM((L, M, RHS), bf16),
@@ -464,7 +626,7 @@
         ],
         name="down",
         cost_estimate=pl.CostEstimate(flops=10**9, bytes_accessed=10**7, transcendentals=0),
-    )(parts, v_rows, near)
+    )(pltpu.with_memory_space_constraint(parts, pltpu.VMEM), v_rows, near)
     return potential.reshape(L * M, RHS)
 
 

time: 124 us -> 123 us (level)
  blocking collectives: 45.3 us -> 0 us
  waiting for transfers between devices: 0.01 us -> 26.7 us
  starting transfers between devices: 12 us -> 26.5 us
  Pallas kernels: 59.4 us -> 67.6 us
  local copies, waits for them, and re-layouts: 6.17 us -> 0.7 us
    all_to_all x1 -> x0, blocking collectives: 45.3 us -> none  [all_steps(): mine = lax.all_to_all(message, LEAF[:3], 0, 0, tiled=True)]
    all_to_all x0 -> x1, waiting for transfers between devices: none -> 26.7 us  [all_steps(): mine = lax.all_to_all(message, LEAF[:3], 0, 0, tiled=True)]
    pallas_call x1 -> x2, Pallas kernels: 2.77 us -> 16 us  [the longest x1 12.4 us: all_steps(): pl.pallas_call(own_kernel, out_shape=jax.ShapeDtypeStruct((L, M, RHS), f3...]
    all_to_all x0 -> x1, starting transfers between devices: none -> 13.1 us  [all_steps(): mine = lax.all_to_all(message, LEAF[:3], 0, 0, tiled=True)]
    unnamed x21 -> x3, local copies, waits for them, and re-layouts: 4.84 us -> 0.7 us
    pallas_call x1, Pallas kernels: 36.5 us -> 32.7 us  [all_steps(): pl.pallas_call(near_kernel, out_shape=jax.ShapeDtypeStruct((L, M, RHS), f...]
    ppermute x1, starting transfers between devices: 1.43 us -> 2.73 us  [all_steps(): before = lax.ppermute(halo, LEAF, up)]
  transfers between devices with their start and end apart: 4 -> 5, of which waited for: 0 -> 1; matrix products, arithmetic and copies ran while one was open for 3% -> 1% of each run, Pallas kernels for 39% -> 46%
where the time goes in v2:
time: 123 us; the launch traced here: 122 us
  Pallas kernels  67.6 us (55%)
  waiting for transfers between devices  26.7 us (22%)
  starting transfers between devices  26.5 us (22%)
    pallas_call x1, Pallas kernels, all_steps(): pl.pallas_call(near_kernel, out_shape=jax.ShapeDtypeStruct((L, M, RHS), f...  32.7 us
    all_to_all x1, waiting for transfers between devices, all_steps(): mine = lax.all_to_all(message, LEAF[:3], 0, 0, tiled=True)  26.7 us
    all_to_all x1, starting transfers between devices, all_steps(): mine = lax.all_to_all(message, LEAF[:3], 0, 0, tiled=True)  13.1 us
    pallas_call x1, Pallas kernels, all_steps(): pl.pallas_call(own_kernel, out_shape=jax.ShapeDtypeStruct((L, M, RHS), f3...  12.4 us
    all_to_all x1, starting transfers between devices, all_steps(): parts = lax.all_to_all(partial, LEAF, 0, 0, tiled=True)  9.34 us
    pallas_call x1, Pallas kernels, all_steps(): pl.pallas_call(up_kernel, out_shape=(jax.ShapeDtypeStruct((CHIPS, MSG, RH...  7.65 us
    pallas_call x1, Pallas kernels, all_steps(): pl.pallas_call(couple_kernel, out_shape=jax.ShapeDtypeStruct((NBASE, K, R...  7.49 us
    pallas_call x1, Pallas kernels, all_steps(): pl.pallas_call(down_kernel, out_shape=jax.ShapeDtypeStruct((L, M, RHS), b...  3.79 us
  transfers between devices with their start and end apart: 5, of which 1 were waited for; matrix products, arithmetic and copies ran while one was open for 1% of the time, Pallas kernels for 46%

profile of v2, /device:TPU:0, one launch (start us, length us, event | category | flops | bytes accessed | tf_op | source)
XLA Modules:
  0.0 121.7 jit_solution(5371342916117385279)
XLA Ops:
  0.0 0.0 copy-start
  0.0 7.6 %up.1 = (bf16[64,48,128]{2,1,0:T(8,128)(2,1)}, bf16[16,128,128]{2,1,0:T(8,128)(2,1)}, bf16[8768,128]{1,0:T(8,128)(2,1)}) custom-call(bf16[8192,128]{1,0:T(8,128)(2,1)} %own.3, f32[3,8192]{1,0:T(4,128)} %coords.3, bf16[64,4096]{1,0:T(8,128)(2,1)} %basis.1, bf16[64,1024]{1,0:T(8,128)(2,1)} %leaf_rows.1, bf16[8,1024]{1,0:T(8,128)(2,1)} %mid_rows.1, ...), custom_call_target="tpu_custom_call" | custom-call | flops 2000000000 | bytes 5000000 | tf_op jit(solution)/shard_map/up/pallas_call | solution.py:498
  7.7 2.7 %collective-permute-start.1 = (bf16[8768,128]{1,0:T(8,128)(2,1)}, bf16[8768,128]{1,0:T(8,128)(2,1)}, u32[]{:S(2)}, u32[]{:S(2)}) collective-permute-start(bf16[8768,128]{1,0:T(8,128)(2,1)} %get-tuple-element.18), channel_id=1, source_target_pairs={{0,1},{1,2},{2,3},{3,4},{4,5},{5,6},{6,7},{7,8},{8,9},{9,10},{10,1... | collective-permute-start | bytes 6733832 | tf_op jit(solution)/shard_map/ppermute | solution.py:521
  10.4 1.3 %collective-permute-start.2 = (bf16[8768,128]{1,0:T(8,128)(2,1)}, bf16[8768,128]{1,0:T(8,128)(2,1)}, u32[]{:S(2)}, u32[]{:S(2)}) collective-permute-start(bf16[8768,128]{1,0:T(8,128)(2,1)} %get-tuple-element.18), channel_id=1, source_target_pairs={{1,0},{2,1},{3,2},{4,3},{5,4},{6,5},{7,6},{8,7},{9,8},{10,9},{11,1... | collective-permute-start | bytes 6733832 | tf_op jit(solution)/shard_map/ppermute | solution.py:522
  11.7 13.1 %all-to-all-start = ((bf16[64,48,128]{2,1,0:T(8,128)(2,1)}), bf16[64,48,128]{2,1,0:T(8,128)(2,1)S(1)}, u32[]{:S(2)}, u32[]{:S(2)}) async-start(bf16[64,48,128]{2,1,0:T(8,128)(2,1)} %get-tuple-element.13), calls=%async_computation | async-start | bytes 1572864 | tf_op jit(solution)/shard_map/all_to_all | solution.py:519
  24.8 0.0 copy-done
  24.8 0.7 copy.14.near_leaves
  25.5 3.6 %early.1 = (s32[64,128]{1,0:T(8,128)}, s32[8,256]{1,0:T(8,128)}, bf16[64,48,128]{2,1,0:T(8,128)(2,1)}, bf16[64,48,128]{2,1,0:T(8,128)(2,1)}) custom-call(s32[64,27]{1,0:T(8,128)} %copy.14.near_leaves, s32[1,189]{1,0:T(1,128)} %bitcast.3, f32[3,8192]{1,0:T(4,128)} %coords.3), custom_call_target="tpu_custom_call" | custom-call | flops 1000000000 | bytes 1000000 | tf_op jit(solution)/shard_map/early/pallas_call | solution.py:524
  29.1 26.7 %all-to-all-done.mine = bf16[64,48,128]{2,1,0:T(8,128)(2,1)S(1)} async-done(((bf16[64,48,128]{2,1,0:T(8,128)(2,1)}), bf16[64,48,128]{2,1,0:T(8,128)(2,1)S(1)}, u32[]{:S(2)}, u32[]{:S(2)}) %all-to-all-start) | async-done | bytes 786464 | tf_op jit(solution)/shard_map/all_to_all | solution.py:519
  55.7 0.0 collective-permute-start
  55.7 12.4 %own.2.so_far = f32[64,128,128]{2,1,0:T(8,128)} custom-call(s32[64,128]{1,0:T(8,128)} %get-tuple-element.15.columns, bf16[64,48,128]{2,1,0:T(8,128)(2,1)} %get-tuple-element.16.own_feats, bf16[64,48,128]{2,1,0:T(8,128)(2,1)} %get-tuple-element.17.own_aims, bf16[8192,128]{1,0:T(8,128)(2,1)} %own.3), custom_call_target="tpu_custom_call" | custom-call | flops 10000000000 | bytes 10000000 | tf_op jit(solution)/shard_map/own/pallas_call | solution.py:573
  68.2 0.0 collective-permute-done.other
  68.2 7.5 %couple.1 = bf16[128,32,128]{2,1,0:T(8,128)(2,1)} custom-call(s32[1]{0:T(128)} %bitcast.core, s32[8,256]{1,0:T(8,128)} %get-tuple-element.12.table, s32[189]{0:T(256)} %sources.1, s32[8]{0:T(128)} %top_target.1, s32[8]{0:T(128)} %top_source.1, bf16[64,48,128]{2,1,0:T(8,128)(2,1)S(1)} %all-to-all-done.mine, ...), custom_call_target="tpu_custom_call" | custom-call | flops 2000000000 | bytes 5000000 | tf_op jit(solution)/shard_map/couple/pallas_call | solution.py:545
  75.7 9.3 %all-to-all-start.1 = ((bf16[128,32,128]{2,1,0:T(8,128)(2,1)}), bf16[128,32,128]{2,1,0:T(8,128)(2,1)S(1)}, u32[]{:S(2)}, u32[]{:S(2)}) async-start(bf16[128,32,128]{2,1,0:T(8,128)(2,1)} %couple.1), calls=%async_computation.1 | async-start | bytes 2097152 | tf_op jit(solution)/shard_map/all_to_all | solution.py:571
  85.0 0.0 collective-permute-done.1.before
  85.0 0.0 collective-permute-done.2.after
  85.1 32.7 %near.1 = f32[64,128,128]{2,1,0:T(8,128)} custom-call(s32[64,128]{1,0:T(8,128)} %get-tuple-element.15.columns, s32[8,256]{1,0:T(8,128)} %get-tuple-element.12.table, bf16[64,48,128]{2,1,0:T(8,128)(2,1)} %get-tuple-element.16.own_feats, bf16[64,48,128]{2,1,0:T(8,128)(2,1)} %get-tuple-element.17.own_aims, bf16[8768,128]{1,0:T(8,128)(2,1)} %collective-permute-done.1.before, ...), custom_call_target="tpu_custom_call" | custom-call | flops 40000000000 | bytes 10000000 | tf_op jit(solution)/shard_map/near/pallas_call | solution.py:592
  117.8 0.0 all-to-all-done.1.parts
  117.8 3.8 %down.1 = bf16[64,128,128]{2,1,0:T(8,128)(2,1)} custom-call(bf16[128,32,128]{2,1,0:T(8,128)(2,1)S(1)} %all-to-all-done.1.parts, bf16[16,128,128]{2,1,0:T(8,128)(2,1)} %get-tuple-element.14.v_rows, f32[64,128,128]{2,1,0:T(8,128)} %near.1), custom_call_target="tpu_custom_call" | custom-call | flops 1000000000 | bytes 10000000 | tf_op jit(solution)/shard_map/down/pallas_call | solution.py:616
Async XLA Ops:
  0.0 24.8 %copy-start = (s32[64,27]{0,1:T(8,128)S(1)}, s32[64,27]{0,1:T(8,128)}, u32[]{:S(2)}) copy-start(s32[64,27]{0,1:T(8,128)} %param.15) | copy-start | bytes 20740
  7.7 77.4 %collective-permute-start.1 = (bf16[8768,128]{1,0:T(8,128)(2,1)}, bf16[8768,128]{1,0:T(8,128)(2,1)}, u32[]{:S(2)}, u32[]{:S(2)}) collective-permute-start(bf16[8768,128]{1,0:T(8,128)(2,1)} %get-tuple-element.18), channel_id=1, source_target_pairs={{0,1},{1,2},{2,3},{3,4},{4,5},{5,6},{6,7},{7,8},{8,9},{9,10},{10,1... | collective-permute-start | bytes 6733832 | tf_op jit(solution)/shard_map/ppermute | solution.py:521
  10.4 74.7 %collective-permute-start.2 = (bf16[8768,128]{1,0:T(8,128)(2,1)}, bf16[8768,128]{1,0:T(8,128)(2,1)}, u32[]{:S(2)}, u32[]{:S(2)}) collective-permute-start(bf16[8768,128]{1,0:T(8,128)(2,1)} %get-tuple-element.18), channel_id=1, source_target_pairs={{1,0},{2,1},{3,2},{4,3},{5,4},{6,5},{7,6},{8,7},{9,8},{10,9},{11,1... | collective-permute-start | bytes 6733832 | tf_op jit(solution)/shard_map/ppermute | solution.py:522
  11.7 44.0 %all-to-all-start = ((bf16[64,48,128]{2,1,0:T(8,128)(2,1)}), bf16[64,48,128]{2,1,0:T(8,128)(2,1)S(1)}, u32[]{:S(2)}, u32[]{:S(2)}) async-start(bf16[64,48,128]{2,1,0:T(8,128)(2,1)} %get-tuple-element.13), calls=%async_computation | async-start | bytes 1572864 | tf_op jit(solution)/shard_map/all_to_all | solution.py:519
  55.7 12.5 %collective-permute-start = (bf16[64,48,128]{2,1,0:T(8,128)(2,1)S(1)}, bf16[64,48,128]{2,1,0:T(8,128)(2,1)S(1)}, u32[]{:S(2)}, u32[]{:S(2)}) collective-permute-start(bf16[64,48,128]{2,1,0:T(8,128)(2,1)S(1)} %all-to-all-done.mine), channel_id=1, source_target_pairs={{0,1},{1,0},{2,3},{3,2},{4,5},{5,4},{6,7},{7,6},{8,9},{9,8},{10,11... | collective-permute-start | bytes 2359304 | tf_op jit(solution)/shard_map/ppermute | solution.py:520
  75.7 42.1 %all-to-all-start.1 = ((bf16[128,32,128]{2,1,0:T(8,128)(2,1)}), bf16[128,32,128]{2,1,0:T(8,128)(2,1)S(1)}, u32[]{:S(2)}, u32[]{:S(2)}) async-start(bf16[128,32,128]{2,1,0:T(8,128)(2,1)} %couple.1), calls=%async_computation.1 | async-start | bytes 2097152 | tf_op jit(solution)/shard_map/all_to_all | solution.py:571

commit v3 on v2

--- a/solution.py
+++ b/solution.py
@@ -22,7 +22,8 @@
 FEAT = 48
 OWN = 6
 REST = NNEAR - OWN
-UNITS = 8
+UNITS = 4
+BATCH = 4
 SPARE = 40
 POINTS = 8192
 TAIL = 576
@@ -347,8 +348,8 @@
     feats[L] = feats[0]
 
     def weigh(batch, store):
-        for u in range(8):
-            l = jnp.minimum(8 * batch + u, L - 1)
+        for u in range(BATCH):
+            l = jnp.minimum(BATCH * batch + u, L - 1)
             for j in range(0, OWN, 2):
                 theirs = jnp.concatenate([feats[columns[l, j]], feats[columns[l, j + 1]]], axis=1)
                 squares = lax.dot_general(
@@ -357,12 +358,12 @@
                 store[u, :, pl.ds(j * M, 2 * M)] = lax.rsqrt(squares).astype(bf16)
 
     def apply(batch, store):
-        for u in range(8):
-            l = 8 * batch + u
+        for u in range(BATCH):
+            l = BATCH * batch + u
             starts = [pl.multiple_of(columns[l, j] * M, M) for j in range(OWN)]
             named = jnp.concatenate([pool[pl.ds(start, M)] for start in starts], axis=0)
             done[l] = jnp.dot(store[u], named, preferred_element_type=f32)
-        part = pl.ds(8 * batch, 8)
+        part = pl.ds(BATCH * batch, BATCH)
         pltpu.make_async_copy(done.at[part], out.at[part], sems.at[3]).start()
 
     weigh(0, kernel_a)
@@ -374,7 +375,7 @@
         apply(2 * i + 1, kernel_b)
         return carry
 
-    lax.fori_loop(0, L // 16, two, 0)
+    lax.fori_loop(0, L // (2 * BATCH), two, 0, unroll=2)
     pltpu.make_async_copy(done, out, sems.at[3]).wait()
 
 
@@ -579,8 +580,8 @@
             pltpu.VMEM((POINTS + M, RHS), bf16),
             pltpu.VMEM((L + 1, FEAT, M), bf16),
             pltpu.VMEM((L, FEAT, M), bf16),
-            pltpu.VMEM((8, M, OWN * M), bf16),
-            pltpu.VMEM((8, M, OWN * M), bf16),
+            pltpu.VMEM((BATCH, M, OWN * M), bf16),
+            pltpu.VMEM((BATCH, M, OWN * M), bf16),
             pltpu.VMEM((L, M, RHS), f32),
             pltpu.SemaphoreType.DMA((4,)),
         ],

time: 123 us -> 122 us (level)
  no operation moved by 1% of the time
where the time goes in v3:
time: 122 us; the launch traced here: 121 us
  Pallas kernels  66.9 us (55%)
  waiting for transfers between devices  26.7 us (22%)
  starting transfers between devices  26.5 us (22%)
    pallas_call x1, Pallas kernels, all_steps(): pl.pallas_call(near_kernel, out_shape=jax.ShapeDtypeStruct((L, M, RHS), f...  32.4 us
    all_to_all x1, waiting for transfers between devices, all_steps(): mine = lax.all_to_all(message, LEAF[:3], 0, 0, tiled=True)  26.7 us
    all_to_all x1, starting transfers between devices, all_steps(): mine = lax.all_to_all(message, LEAF[:3], 0, 0, tiled=True)  13.1 us
    pallas_call x1, Pallas kernels, all_steps(): pl.pallas_call(own_kernel, out_shape=jax.ShapeDtypeStruct((L, M, RHS), f3...  12 us
    all_to_all x1, starting transfers between devices, all_steps(): parts = lax.all_to_all(partial, LEAF, 0, 0, tiled=True)  9.35 us
    pallas_call x1, Pallas kernels, all_steps(): pl.pallas_call(up_kernel, out_shape=(jax.ShapeDtypeStruct((CHIPS, MSG, RH...  7.65 us
    pallas_call x1, Pallas kernels, all_steps(): pl.pallas_call(couple_kernel, out_shape=jax.ShapeDtypeStruct((NBASE, K, R...  7.49 us
    pallas_call x1, Pallas kernels, all_steps(): pl.pallas_call(down_kernel, out_shape=jax.ShapeDtypeStruct((L, M, RHS), b...  3.79 us
  transfers between devices with their start and end apart: 5, of which 1 were waited for; matrix products, arithmetic and copies ran while one was open for 1% of the time, Pallas kernels for 46%

profile of v3, /device:TPU:0, one launch (start us, length us, event | category | flops | bytes accessed | tf_op | source)
XLA Modules:
  0.0 121.0 jit_solution(13237505630079793706)
XLA Ops:
  0.0 0.0 copy-start
  0.0 7.6 %up.1 = (bf16[64,48,128]{2,1,0:T(8,128)(2,1)}, bf16[16,128,128]{2,1,0:T(8,128)(2,1)}, bf16[8768,128]{1,0:T(8,128)(2,1)}) custom-call(bf16[8192,128]{1,0:T(8,128)(2,1)} %own.3, f32[3,8192]{1,0:T(4,128)} %coords.3, bf16[64,4096]{1,0:T(8,128)(2,1)} %basis.1, bf16[64,1024]{1,0:T(8,128)(2,1)} %leaf_rows.1, bf16[8,1024]{1,0:T(8,128)(2,1)} %mid_rows.1, ...), custom_call_target="tpu_custom_call" | custom-call | flops 2000000000 | bytes 5000000 | tf_op jit(solution)/shard_map/up/pallas_call | solution.py:499
  7.7 2.7 %collective-permute-start.1 = (bf16[8768,128]{1,0:T(8,128)(2,1)}, bf16[8768,128]{1,0:T(8,128)(2,1)}, u32[]{:S(2)}, u32[]{:S(2)}) collective-permute-start(bf16[8768,128]{1,0:T(8,128)(2,1)} %get-tuple-element.18), channel_id=1, source_target_pairs={{0,1},{1,2},{2,3},{3,4},{4,5},{5,6},{6,7},{7,8},{8,9},{9,10},{10,1... | collective-permute-start | bytes 6733832 | tf_op jit(solution)/shard_map/ppermute | solution.py:522
  10.4 1.3 %collective-permute-start.2 = (bf16[8768,128]{1,0:T(8,128)(2,1)}, bf16[8768,128]{1,0:T(8,128)(2,1)}, u32[]{:S(2)}, u32[]{:S(2)}) collective-permute-start(bf16[8768,128]{1,0:T(8,128)(2,1)} %get-tuple-element.18), channel_id=1, source_target_pairs={{1,0},{2,1},{3,2},{4,3},{5,4},{6,5},{7,6},{8,7},{9,8},{10,9},{11,1... | collective-permute-start | bytes 6733832 | tf_op jit(solution)/shard_map/ppermute | solution.py:523
  11.7 13.1 %all-to-all-start = ((bf16[64,48,128]{2,1,0:T(8,128)(2,1)}), bf16[64,48,128]{2,1,0:T(8,128)(2,1)S(1)}, u32[]{:S(2)}, u32[]{:S(2)}) async-start(bf16[64,48,128]{2,1,0:T(8,128)(2,1)} %get-tuple-element.13), calls=%async_computation | async-start | bytes 1572864 | tf_op jit(solution)/shard_map/all_to_all | solution.py:520
  24.8 0.0 copy-done
  24.8 0.7 copy.14.near_leaves
  25.5 3.6 %early.1 = (s32[64,128]{1,0:T(8,128)}, s32[8,256]{1,0:T(8,128)}, bf16[64,48,128]{2,1,0:T(8,128)(2,1)}, bf16[64,48,128]{2,1,0:T(8,128)(2,1)}) custom-call(s32[64,27]{1,0:T(8,128)} %copy.14.near_leaves, s32[1,189]{1,0:T(1,128)} %bitcast.3, f32[3,8192]{1,0:T(4,128)} %coords.3), custom_call_target="tpu_custom_call" | custom-call | flops 1000000000 | bytes 1000000 | tf_op jit(solution)/shard_map/early/pallas_call | solution.py:525
  29.1 26.7 %all-to-all-done.mine = bf16[64,48,128]{2,1,0:T(8,128)(2,1)S(1)} async-done(((bf16[64,48,128]{2,1,0:T(8,128)(2,1)}), bf16[64,48,128]{2,1,0:T(8,128)(2,1)S(1)}, u32[]{:S(2)}, u32[]{:S(2)}) %all-to-all-start) | async-done | bytes 786464 | tf_op jit(solution)/shard_map/all_to_all | solution.py:520
  55.7 0.0 collective-permute-start
  55.7 12.0 %own.2.so_far = f32[64,128,128]{2,1,0:T(8,128)} custom-call(s32[64,128]{1,0:T(8,128)} %get-tuple-element.15.columns, bf16[64,48,128]{2,1,0:T(8,128)(2,1)} %get-tuple-element.16.own_feats, bf16[64,48,128]{2,1,0:T(8,128)(2,1)} %get-tuple-element.17.own_aims, bf16[8192,128]{1,0:T(8,128)(2,1)} %own.3), custom_call_target="tpu_custom_call" | custom-call | flops 10000000000 | bytes 10000000 | tf_op jit(solution)/shard_map/own/pallas_call | solution.py:574
  67.7 0.0 collective-permute-done.other
  67.7 7.5 %couple.1 = bf16[128,32,128]{2,1,0:T(8,128)(2,1)} custom-call(s32[1]{0:T(128)} %bitcast.core, s32[8,256]{1,0:T(8,128)} %get-tuple-element.12.table, s32[189]{0:T(256)} %sources.1, s32[8]{0:T(128)} %top_target.1, s32[8]{0:T(128)} %top_source.1, bf16[64,48,128]{2,1,0:T(8,128)(2,1)S(1)} %all-to-all-done.mine, ...), custom_call_target="tpu_custom_call" | custom-call | flops 2000000000 | bytes 5000000 | tf_op jit(solution)/shard_map/couple/pallas_call | solution.py:546
  75.2 9.3 %all-to-all-start.1 = ((bf16[128,32,128]{2,1,0:T(8,128)(2,1)}), bf16[128,32,128]{2,1,0:T(8,128)(2,1)S(1)}, u32[]{:S(2)}, u32[]{:S(2)}) async-start(bf16[128,32,128]{2,1,0:T(8,128)(2,1)} %couple.1), calls=%async_computation.1 | async-start | bytes 2097152 | tf_op jit(solution)/shard_map/all_to_all | solution.py:572
  84.6 0.0 collective-permute-done.1.before
  84.6 0.0 collective-permute-done.2.after
  84.6 32.4 %near.1 = f32[64,128,128]{2,1,0:T(8,128)} custom-call(s32[64,128]{1,0:T(8,128)} %get-tuple-element.15.columns, s32[8,256]{1,0:T(8,128)} %get-tuple-element.12.table, bf16[64,48,128]{2,1,0:T(8,128)(2,1)} %get-tuple-element.16.own_feats, bf16[64,48,128]{2,1,0:T(8,128)(2,1)} %get-tuple-element.17.own_aims, bf16[8768,128]{1,0:T(8,128)(2,1)} %collective-permute-done.1.before, ...), custom_call_target="tpu_custom_call" | custom-call | flops 40000000000 | bytes 10000000 | tf_op jit(solution)/shard_map/near/pallas_call | solution.py:593
  117.0 0.0 all-to-all-done.1.parts
  117.0 3.8 %down.1 = bf16[64,128,128]{2,1,0:T(8,128)(2,1)} custom-call(bf16[128,32,128]{2,1,0:T(8,128)(2,1)S(1)} %all-to-all-done.1.parts, bf16[16,128,128]{2,1,0:T(8,128)(2,1)} %get-tuple-element.14.v_rows, f32[64,128,128]{2,1,0:T(8,128)} %near.1), custom_call_target="tpu_custom_call" | custom-call | flops 1000000000 | bytes 10000000 | tf_op jit(solution)/shard_map/down/pallas_call | solution.py:617
Async XLA Ops:
  0.0 24.8 %copy-start = (s32[64,27]{0,1:T(8,128)S(1)}, s32[64,27]{0,1:T(8,128)}, u32[]{:S(2)}) copy-start(s32[64,27]{0,1:T(8,128)} %param.15) | copy-start | bytes 20740
  7.7 76.9 %collective-permute-start.1 = (bf16[8768,128]{1,0:T(8,128)(2,1)}, bf16[8768,128]{1,0:T(8,128)(2,1)}, u32[]{:S(2)}, u32[]{:S(2)}) collective-permute-start(bf16[8768,128]{1,0:T(8,128)(2,1)} %get-tuple-element.18), channel_id=1, source_target_pairs={{0,1},{1,2},{2,3},{3,4},{4,5},{5,6},{6,7},{7,8},{8,9},{9,10},{10,1... | collective-permute-start | bytes 6733832 | tf_op jit(solution)/shard_map/ppermute | solution.py:522
  10.4 74.2 %collective-permute-start.2 = (bf16[8768,128]{1,0:T(8,128)(2,1)}, bf16[8768,128]{1,0:T(8,128)(2,1)}, u32[]{:S(2)}, u32[]{:S(2)}) collective-permute-start(bf16[8768,128]{1,0:T(8,128)(2,1)} %get-tuple-element.18), channel_id=1, source_target_pairs={{1,0},{2,1},{3,2},{4,3},{5,4},{6,5},{7,6},{8,7},{9,8},{10,9},{11,1... | collective-permute-start | bytes 6733832 | tf_op jit(solution)/shard_map/ppermute | solution.py:523
  11.7 44.0 %all-to-all-start = ((bf16[64,48,128]{2,1,0:T(8,128)(2,1)}), bf16[64,48,128]{2,1,0:T(8,128)(2,1)S(1)}, u32[]{:S(2)}, u32[]{:S(2)}) async-start(bf16[64,48,128]{2,1,0:T(8,128)(2,1)} %get-tuple-element.13), calls=%async_computation | async-start | bytes 1572864 | tf_op jit(solution)/shard_map/all_to_all | solution.py:520
  55.7 12.0 %collective-permute-start = (bf16[64,48,128]{2,1,0:T(8,128)(2,1)S(1)}, bf16[64,48,128]{2,1,0:T(8,128)(2,1)S(1)}, u32[]{:S(2)}, u32[]{:S(2)}) collective-permute-start(bf16[64,48,128]{2,1,0:T(8,128)(2,1)S(1)} %all-to-all-done.mine), channel_id=1, source_target_pairs={{0,1},{1,0},{2,3},{3,2},{4,5},{5,4},{6,7},{7,6},{8,9},{9,8},{10,11... | collective-permute-start | bytes 2359304 | tf_op jit(solution)/shard_map/ppermute | solution.py:521
  75.2 41.8 %all-to-all-start.1 = ((bf16[128,32,128]{2,1,0:T(8,128)(2,1)}), bf16[128,32,128]{2,1,0:T(8,128)(2,1)S(1)}, u32[]{:S(2)}, u32[]{:S(2)}) async-start(bf16[128,32,128]{2,1,0:T(8,128)(2,1)} %couple.1), calls=%async_computation.1 | async-start | bytes 2097152 | tf_op jit(solution)/shard_map/all_to_all | solution.py:572
